TPU v7x, 128 devices: a whole 4x4x4 slice. The times are simulated.
128 devices in a mesh: row: 32 (over x, z, core), col: 4 (over y).
Axes of the slice: x: 4, y: 4, z: 4, core: 2. Of those that a mesh axis runs over, the one named last changes fastest.
Arguments:
- graph_one: bfloat16 [16384, 16384], P('row'), may hold values from -64 to 64
- graph_two: bfloat16 [2048, 2048], P('col'), may hold values from -64 to 64
- coupling: float32 [16384, 2048], P('row', 'col'), may hold values from 0.2 to 5
- sizes_one: int32 [32], replicated, may hold values from 256 to 512
- sizes_two: int32 [4], replicated, may hold values from 256 to 512
Outputs:
- new_coupling: float32 [16384, 2048], P('row', 'col')
- row_potential: float32 [16384], P('row')
- col_potential: float32 [2048], P('col')
All inputs are finite; a program needn't handle non-finite values.
Results may differ from a plain program's by a relative error of at most 0.007.
The roundings to bfloat16 on the way count: a program that leaves them out, or rounds other values in their place, can miss the bound.
Values may be sent and summed in bfloat16 or wider, within the bound.
A program may use at most 128 MiB of HBM per device.

v0:
```python
import math

import jax
import jax.numpy as jnp
from jax import lax
from jax.sharding import PartitionSpec as P

BLOCK = 512
SWEEPS = 5


very_low = -1e30


def copy_for_each(shard, axis):
    copies = jnp.broadcast_to(shard, (lax.axis_size(axis), *shard.shape))
    return lax.all_to_all(copies, axis, split_axis=0, concat_axis=0, tiled=True)


def taken_together(shard, axis):
    return copy_for_each(shard, axis).max(axis=0)


def of_everyone(shard, axis):
    return copy_for_each(shard, axis).sum(axis=0)


def in_order(blocks, dim):
    blocks = jnp.moveaxis(blocks, 0, dim)
    lengths = blocks.shape
    return blocks.reshape(*lengths[:dim], lengths[dim] * lengths[dim + 1], *lengths[dim + 2 :])


def gather_directly(shard, axis, dim):
    return in_order(copy_for_each(shard, axis), dim)


def live_slots(sizes, count):
    return jnp.arange(count, dtype=jnp.int32) % BLOCK < jnp.repeat(
        sizes, BLOCK, total_repeat_length=count
    )


def across_columns(values, keep_mask):
    masked = jnp.where(keep_mask[None, :], values, very_low)
    highest = jnp.max(masked, axis=1)
    summed = jnp.sum(jnp.where(keep_mask[None, :], jnp.exp(masked - highest[:, None]), 0.0), axis=1)
    overall = taken_together(highest, "col")
    summed = of_everyone(summed * jnp.exp(highest - overall), "col")
    highest = overall
    return highest + jnp.log(summed)


def across_rows(values, keep_mask):
    masked = jnp.where(keep_mask[:, None], values, very_low)
    highest = jnp.max(masked, axis=0)
    summed = jnp.sum(jnp.where(keep_mask[:, None], jnp.exp(masked - highest[None, :]), 0.0), axis=0)
    overall = taken_together(highest, "row")
    summed = of_everyone(summed * jnp.exp(highest - overall), "row")
    highest = overall
    return highest + jnp.log(summed)


def body(graph_one, graph_two, coupling, sizes_one, sizes_two):
    local_rows = graph_one.shape[0]
    count_one = graph_one.shape[1]
    local_cols = graph_two.shape[0]
    count_two = graph_two.shape[1]
    row_begin = lax.axis_index("row") * local_rows
    col_begin = lax.axis_index("col") * local_cols
    all_one = live_slots(sizes_one, count_one)
    all_two = live_slots(sizes_two, count_two)
    live_rows = lax.dynamic_slice_in_dim(all_one, row_begin, local_rows)
    live_cols = lax.dynamic_slice_in_dim(all_two, col_begin, local_cols)
    total_one = jnp.sum(sizes_one).astype(jnp.float32)
    total_two = jnp.sum(sizes_two).astype(jnp.float32)
    live_both = live_rows[:, None] & live_cols[None, :]
    rounded_plan = jnp.where(live_both, coupling, jnp.float32(0.0)).astype(jnp.bfloat16)
    start_value = jnp.zeros((local_rows, local_cols), jnp.float32)
    shard_piece = lax.all_gather(rounded_plan, "row", axis=0, tiled=True)
    columns = lax.slice_in_dim(graph_one, 0, shard_piece.shape[0], axis=1)
    first_float = start_value + jnp.dot(columns, shard_piece, preferred_element_type=jnp.float32)
    first_product = first_float.astype(jnp.bfloat16)
    whole_first = gather_directly(first_product, "col", 1)
    cross_term = lax.dot_general(
        whole_first, graph_two, (((1,), (1,)), ((), ())), preferred_element_type=jnp.float32
    )
    row_const = (
        jnp.sum(
            jnp.square(graph_one.astype(jnp.float32)) * all_one.astype(jnp.float32)[None, :], axis=1
        )
        / total_one
    )
    col_const = (
        jnp.sum(
            jnp.square(graph_two.astype(jnp.float32)) * all_two.astype(jnp.float32)[None, :], axis=1
        )
        / total_two
    )
    mass_scale = float(count_one * count_two)
    epsilon = 1.0 / math.sqrt(mass_scale)
    reduced_cost = -2.0 / mass_scale * cross_term
    reduced_col = jnp.zeros((local_cols,), jnp.float32)
    reduced_row = jnp.zeros((local_rows,), jnp.float32)
    for sweep_index in range(SWEEPS):
        row_lse = across_columns((reduced_col[None, :] - reduced_cost) / epsilon, live_cols)
        reduced_row = jnp.where(
            live_rows, -epsilon * jnp.log(total_one) - epsilon * row_lse, jnp.float32(0.0)
        )
        col_lse = across_rows((reduced_row[:, None] - reduced_cost) / epsilon, live_rows)
        reduced_col = jnp.where(
            live_cols, -epsilon * jnp.log(total_two) - epsilon * col_lse, jnp.float32(0.0)
        )
    exponent = (reduced_row[:, None] + reduced_col[None, :] - reduced_cost) / epsilon
    new_coupling = jnp.where(live_both, mass_scale * jnp.exp(exponent), jnp.float32(0.0))
    row_potential = jnp.where(live_rows, reduced_row + row_const, jnp.float32(0.0))
    col_potential = jnp.where(live_cols, reduced_col + col_const, jnp.float32(0.0))
    return (new_coupling, row_potential, col_potential)


def solution(mesh):
    return jax.shard_map(
        body,
        mesh=mesh,
        in_specs=(P("row", None), P("col", None), P("row", "col"), P(), P()),
        out_specs=(P("row", "col"), P("row"), P("col")),
        check_vma=False,
    )
```

profile of v0, /device:TPU:1, one launch (start us, length us, event | category | flops | bytes accessed | tf_op | source)
XLA Modules:
  0.0 387.1 jit_solution(18238070078192399517)
XLA Ops:
  16.1 21.3 %fusion.24 = (f32[16384]{0:T(1024)S(1)}, pred[16384]{0:T(1024)(128)(4,1)S(1)}) fusion(pred[16384]{0:T(1024)(128)(4,1)} %constant.307, pred[16384]{0:T(1024)(128)(4,1)} %constant.308, pred[16384]{0:T(1024)(128)(4,1)} %constant.309, pred[16384]{0:T(1024)(128)(4,1)} %constant.310, pred[16384]{0:T(1024)(128)(4,1)} %constant.311, pred[16384]{0:T(1024)(128)(4,1)} %constant.312, ...), kind=kLoop, calls=%fused_computation.75 | loop fusion | flops 638976 | bytes 589952 | tf_op jit(solution)/shard_map/convert_element_type | solution.py:90
  39.6 76.4 %all-gather.2.cloned.1.call-done = bf16[16384,512]{1,0:T(8,128)(2,1)} async-done(((bf16[512,512]{1,0:T(8,128)(2,1)}), bf16[16384,512]{1,0:T(8,128)(2,1)}) %all-gather.2.cloned.1.call-update) | async-done | bytes 16777232 | tf_op jit(solution)/shard_map/all_gather | solution.py:80
  116.1 17.3 %fusion = bf16[512,512]{0,1:T(8,128)(2,1)S(1)} fusion(bf16[16384,512]{1,0:T(8,128)(2,1)} %all-gather.2.cloned.1.call-done, bf16[512,16384]{1,0:T(8,128)(2,1)} %param.9), kind=kOutput, calls=%fused_computation.6 | convolution fusion | flops 8590196736 | bytes 34078720 | tf_op jit(solution)/shard_map/dot_general | solution.py:82
  133.5 29.8 %all_to_all.125 = bf16[4,512,512]{1,2,0:T(8,128)(2,1)S(1)} all-to-all(bf16[4,512,512]{1,2,0:T(8,128)(2,1)S(1)} %broadcast_in_dim.230), channel_id=1, replica_groups=mesh['row'=32,'col'=4] {'col'}, dimensions={0} | all-to-all | bytes 4194304 | tf_op jit(solution)/shard_map/all_to_all | solution.py:17
  181.8 8.8 %all-to-all-start.3 = ((f32[32,1,512]{2,1,0:T(1,128)}), f32[32,1,512]{2,1,0:T(1,128)S(1)}, u32[]{:S(2)}, u32[]{:S(2)}) async-start(f32[32,1,512]{2,1,0:T(1,128)} %broadcast_in_dim.235), calls=%async_computation.3 | async-start | bytes 131072 | tf_op jit(solution)/shard_map/all_to_all | solution.py:17
  191.0 7.0 %all-to-all-done.3 = f32[32,1,512]{2,1,0:T(1,128)S(1)} async-done(((f32[32,1,512]{2,1,0:T(1,128)}), f32[32,1,512]{2,1,0:T(1,128)S(1)}, u32[]{:S(2)}, u32[]{:S(2)}) %all-to-all-start.3) | async-done | bytes 65568 | tf_op jit(solution)/shard_map/all_to_all | solution.py:17
  204.0 6.1 %all-to-all-done.4 = f32[32,1,512]{2,1,0:T(1,128)S(1)} async-done(((f32[32,1,512]{2,1,0:T(1,128)}), f32[32,1,512]{2,1,0:T(1,128)S(1)}, u32[]{:S(2)}, u32[]{:S(2)}) %all-to-all-start.4) | async-done | bytes 65568 | tf_op jit(solution)/shard_map/all_to_all | solution.py:17
  218.6 6.5 %all_to_all.126 = f32[4,1,512]{2,1,0:T(1,128)S(1)} all-to-all(f32[4,1,512]{2,1,0:T(1,128)S(1)} %broadcast_in_dim.238), channel_id=1, replica_groups=mesh['row'=32,'col'=4] {'col'}, dimensions={0} | all-to-all | bytes 16384 | tf_op jit(solution)/shard_map/all_to_all | solution.py:17
  226.1 6.2 %all-to-all-start.7 = ((f32[32,1,512]{2,1,0:T(1,128)}), f32[32,1,512]{2,1,0:T(1,128)S(1)}, u32[]{:S(2)}, u32[]{:S(2)}) async-start(f32[32,1,512]{2,1,0:T(1,128)} %broadcast_in_dim.239), calls=%async_computation.7 | async-start | bytes 131072 | tf_op jit(solution)/shard_map/all_to_all | solution.py:17
  232.7 7.1 %all-to-all-done.7 = f32[32,1,512]{2,1,0:T(1,128)S(1)} async-done(((f32[32,1,512]{2,1,0:T(1,128)}), f32[32,1,512]{2,1,0:T(1,128)S(1)}, u32[]{:S(2)}, u32[]{:S(2)}) %all-to-all-start.7) | async-done | bytes 65568 | tf_op jit(solution)/shard_map/all_to_all | solution.py:17
  239.9 10.9 %all_to_all.127 = f32[32,1,512]{2,1,0:T(1,128)S(1)} all-to-all(f32[32,1,512]{2,1,0:T(1,128)S(1)} %broadcast_in_dim.240), channel_id=1, replica_groups=mesh['row'=32,'col'=4] {'row'}, dimensions={0} | all-to-all | bytes 131072 | tf_op jit(solution)/shard_map/all_to_all | solution.py:17
  259.2 6.5 %all_to_all.128 = f32[4,1,512]{2,1,0:T(1,128)S(1)} all-to-all(f32[4,1,512]{2,1,0:T(1,128)S(1)} %broadcast_in_dim.242), channel_id=1, replica_groups=mesh['row'=32,'col'=4] {'col'}, dimensions={0} | all-to-all | bytes 16384 | tf_op jit(solution)/shard_map/all_to_all | solution.py:17
  266.7 6.2 %all-to-all-start.11 = ((f32[32,1,512]{2,1,0:T(1,128)}), f32[32,1,512]{2,1,0:T(1,128)S(1)}, u32[]{:S(2)}, u32[]{:S(2)}) async-start(f32[32,1,512]{2,1,0:T(1,128)} %broadcast_in_dim.243), calls=%async_computation.11 | async-start | bytes 131072 | tf_op jit(solution)/shard_map/all_to_all | solution.py:17
  273.3 7.1 %all-to-all-done.11 = f32[32,1,512]{2,1,0:T(1,128)S(1)} async-done(((f32[32,1,512]{2,1,0:T(1,128)}), f32[32,1,512]{2,1,0:T(1,128)S(1)}, u32[]{:S(2)}, u32[]{:S(2)}) %all-to-all-start.11) | async-done | bytes 65568 | tf_op jit(solution)/shard_map/all_to_all | solution.py:17
  280.5 10.9 %all_to_all.129 = f32[32,1,512]{2,1,0:T(1,128)S(1)} all-to-all(f32[32,1,512]{2,1,0:T(1,128)S(1)} %broadcast_in_dim.244), channel_id=1, replica_groups=mesh['row'=32,'col'=4] {'row'}, dimensions={0} | all-to-all | bytes 131072 | tf_op jit(solution)/shard_map/all_to_all | solution.py:17
  299.8 6.5 %all_to_all.130 = f32[4,1,512]{2,1,0:T(1,128)S(1)} all-to-all(f32[4,1,512]{2,1,0:T(1,128)S(1)} %broadcast_in_dim.246), channel_id=1, replica_groups=mesh['row'=32,'col'=4] {'col'}, dimensions={0} | all-to-all | bytes 16384 | tf_op jit(solution)/shard_map/all_to_all | solution.py:17
  307.3 6.2 %all-to-all-start.15 = ((f32[32,1,512]{2,1,0:T(1,128)}), f32[32,1,512]{2,1,0:T(1,128)S(1)}, u32[]{:S(2)}, u32[]{:S(2)}) async-start(f32[32,1,512]{2,1,0:T(1,128)} %broadcast_in_dim.247), calls=%async_computation.15 | async-start | bytes 131072 | tf_op jit(solution)/shard_map/all_to_all | solution.py:17
  313.9 7.1 %all-to-all-done.15 = f32[32,1,512]{2,1,0:T(1,128)S(1)} async-done(((f32[32,1,512]{2,1,0:T(1,128)}), f32[32,1,512]{2,1,0:T(1,128)S(1)}, u32[]{:S(2)}, u32[]{:S(2)}) %all-to-all-start.15) | async-done | bytes 65568 | tf_op jit(solution)/shard_map/all_to_all | solution.py:17
  321.1 10.9 %all_to_all.131 = f32[32,1,512]{2,1,0:T(1,128)S(1)} all-to-all(f32[32,1,512]{2,1,0:T(1,128)S(1)} %broadcast_in_dim.248), channel_id=1, replica_groups=mesh['row'=32,'col'=4] {'row'}, dimensions={0} | all-to-all | bytes 131072 | tf_op jit(solution)/shard_map/all_to_all | solution.py:17
  344.3 7.6 %multiply_reduce_fusion = f32[512]{0:T(512)S(1)} fusion(bf16[512,16384]{1,0:T(8,128)(2,1)} %param.9, f32[16384]{0:T(1024)S(1)} %get-tuple-element.33), kind=kLoop, calls=%fused_computation | loop fusion | flops 33553920 | bytes 16844800 | tf_op jit(solution)/shard_map/reduce_sum | solution.py:89
  353.5 5.1 %all-to-all-start.19 = ((f32[32,1,512]{2,1,0:T(1,128)}), f32[32,1,512]{2,1,0:T(1,128)S(1)}, u32[]{:S(2)}, u32[]{:S(2)}) async-start(f32[32,1,512]{2,1,0:T(1,128)} %broadcast_in_dim.251), calls=%async_computation.19 | async-start | bytes 131072 | tf_op jit(solution)/shard_map/all_to_all | solution.py:17
  358.9 7.1 %all-to-all-done.19 = f32[32,1,512]{2,1,0:T(1,128)S(1)} async-done(((f32[32,1,512]{2,1,0:T(1,128)}), f32[32,1,512]{2,1,0:T(1,128)S(1)}, u32[]{:S(2)}, u32[]{:S(2)}) %all-to-all-start.19) | async-done | bytes 65568 | tf_op jit(solution)/shard_map/all_to_all | solution.py:17
  366.7 3.9 %all-to-all-start.20 = ((f32[32,1,512]{2,1,0:T(1,128)}), f32[32,1,512]{2,1,0:T(1,128)S(1)}, u32[]{:S(2)}, u32[]{:S(2)}) async-start(f32[32,1,512]{2,1,0:T(1,128)} %broadcast_in_dim.252), calls=%async_computation.20 | async-start | bytes 131072 | tf_op jit(solution)/shard_map/all_to_all | solution.py:17
  371.3 6.8 %all-to-all-done.20 = f32[32,1,512]{2,1,0:T(1,128)S(1)} async-done(((f32[32,1,512]{2,1,0:T(1,128)}), f32[32,1,512]{2,1,0:T(1,128)S(1)}, u32[]{:S(2)}, u32[]{:S(2)}) %all-to-all-start.20) | async-done | bytes 65568 | tf_op jit(solution)/shard_map/all_to_all | solution.py:17
  (115 shorter events, 82.0 us)
Async XLA Ops:
  7.2 108.9 %all-gather.2.cloned.1.call-start = ((), (), s32[]{:S(2)}) async-start(), calls=%async_computation.21 | async-start | bytes 17301504 | tf_op jit(solution)/shard_map/all_gather | solution.py:80
  133.3 30.0 %copy-start = (bf16[512,2048]{1,0:T(8,128)(2,1)S(1)}, bf16[512,2048]{1,0:T(8,128)(2,1)}, u32[]{:S(2)}) copy-start(bf16[512,2048]{1,0:T(8,128)(2,1)} %param.10) | copy-start | bytes 6291460
  163.3 13.3 %copy-start.1 = (s32[32]{0:T(128)S(1)}, s32[32]{0:T(128)}, u32[]{:S(2)}) copy-start(s32[32]{0:T(128)} %param.12) | copy-start | bytes 388
  163.3 39.3 %copy-start.2 = (s32[4]{0:T(128)S(1)}, s32[4]{0:T(128)}, u32[]{:S(2)}) copy-start(s32[4]{0:T(128)} %param.13) | copy-start | bytes 52
  165.4 7.4 %all-to-all-start.1 = ((f32[4,1,512]{2,1,0:T(1,128)}), f32[4,1,512]{2,1,0:T(1,128)S(1)}, u32[]{:S(2)}, u32[]{:S(2)}) async-start(f32[4,1,512]{2,1,0:T(1,128)} %broadcast_in_dim.232), calls=%async_computation.1 | async-start | bytes 16384 | tf_op jit(solution)/shard_map/all_to_all | solution.py:17
  173.4 7.4 %all-to-all-start.2 = ((f32[4,1,512]{2,1,0:T(1,128)}), f32[4,1,512]{2,1,0:T(1,128)S(1)}, u32[]{:S(2)}, u32[]{:S(2)}) async-start(f32[4,1,512]{2,1,0:T(1,128)} %broadcast_in_dim.233), calls=%async_computation.2 | async-start | bytes 16384 | tf_op jit(solution)/shard_map/all_to_all | solution.py:17
  181.8 16.2 %all-to-all-start.3 = ((f32[32,1,512]{2,1,0:T(1,128)}), f32[32,1,512]{2,1,0:T(1,128)S(1)}, u32[]{:S(2)}, u32[]{:S(2)}) async-start(f32[32,1,512]{2,1,0:T(1,128)} %broadcast_in_dim.235), calls=%async_computation.3 | async-start | bytes 131072 | tf_op jit(solution)/shard_map/all_to_all | solution.py:17
  198.8 11.4 %all-to-all-start.4 = ((f32[32,1,512]{2,1,0:T(1,128)}), f32[32,1,512]{2,1,0:T(1,128)S(1)}, u32[]{:S(2)}, u32[]{:S(2)}) async-start(f32[32,1,512]{2,1,0:T(1,128)} %broadcast_in_dim.236), calls=%async_computation.4 | async-start | bytes 131072 | tf_op jit(solution)/shard_map/all_to_all | solution.py:17
  211.1 7.4 %all-to-all-start.5 = ((f32[4,1,512]{2,1,0:T(1,128)}), f32[4,1,512]{2,1,0:T(1,128)S(1)}, u32[]{:S(2)}, u32[]{:S(2)}) async-start(f32[4,1,512]{2,1,0:T(1,128)} %broadcast_in_dim.237), calls=%async_computation.5 | async-start | bytes 16384 | tf_op jit(solution)/shard_map/all_to_all | solution.py:17
  226.1 13.7 %all-to-all-start.7 = ((f32[32,1,512]{2,1,0:T(1,128)}), f32[32,1,512]{2,1,0:T(1,128)S(1)}, u32[]{:S(2)}, u32[]{:S(2)}) async-start(f32[32,1,512]{2,1,0:T(1,128)} %broadcast_in_dim.239), calls=%async_computation.7 | async-start | bytes 131072 | tf_op jit(solution)/shard_map/all_to_all | solution.py:17
  251.7 7.4 %all-to-all-start.9 = ((f32[4,1,512]{2,1,0:T(1,128)}), f32[4,1,512]{2,1,0:T(1,128)S(1)}, u32[]{:S(2)}, u32[]{:S(2)}) async-start(f32[4,1,512]{2,1,0:T(1,128)} %broadcast_in_dim.241), calls=%async_computation.9 | async-start | bytes 16384 | tf_op jit(solution)/shard_map/all_to_all | solution.py:17
  266.7 13.7 %all-to-all-start.11 = ((f32[32,1,512]{2,1,0:T(1,128)}), f32[32,1,512]{2,1,0:T(1,128)S(1)}, u32[]{:S(2)}, u32[]{:S(2)}) async-start(f32[32,1,512]{2,1,0:T(1,128)} %broadcast_in_dim.243), calls=%async_computation.11 | async-start | bytes 131072 | tf_op jit(solution)/shard_map/all_to_all | solution.py:17
  292.4 7.4 %all-to-all-start.13 = ((f32[4,1,512]{2,1,0:T(1,128)}), f32[4,1,512]{2,1,0:T(1,128)S(1)}, u32[]{:S(2)}, u32[]{:S(2)}) async-start(f32[4,1,512]{2,1,0:T(1,128)} %broadcast_in_dim.245), calls=%async_computation.13 | async-start | bytes 16384 | tf_op jit(solution)/shard_map/all_to_all | solution.py:17
  307.3 13.7 %all-to-all-start.15 = ((f32[32,1,512]{2,1,0:T(1,128)}), f32[32,1,512]{2,1,0:T(1,128)S(1)}, u32[]{:S(2)}, u32[]{:S(2)}) async-start(f32[32,1,512]{2,1,0:T(1,128)} %broadcast_in_dim.247), calls=%async_computation.15 | async-start | bytes 131072 | tf_op jit(solution)/shard_map/all_to_all | solution.py:17
  333.0 7.4 %all-to-all-start.17 = ((f32[4,1,512]{2,1,0:T(1,128)}), f32[4,1,512]{2,1,0:T(1,128)S(1)}, u32[]{:S(2)}, u32[]{:S(2)}) async-start(f32[4,1,512]{2,1,0:T(1,128)} %broadcast_in_dim.249), calls=%async_computation.17 | async-start | bytes 16384 | tf_op jit(solution)/shard_map/all_to_all | solution.py:17
  341.0 10.8 %all-to-all-start.18 = ((f32[4,1,512]{2,1,0:T(1,128)}), f32[4,1,512]{2,1,0:T(1,128)S(1)}, u32[]{:S(2)}, u32[]{:S(2)}) async-start(f32[4,1,512]{2,1,0:T(1,128)} %broadcast_in_dim.250), calls=%async_computation.18 | async-start | bytes 16384 | tf_op jit(solution)/shard_map/all_to_all | solution.py:17
  353.5 12.5 %all-to-all-start.19 = ((f32[32,1,512]{2,1,0:T(1,128)}), f32[32,1,512]{2,1,0:T(1,128)S(1)}, u32[]{:S(2)}, u32[]{:S(2)}) async-start(f32[32,1,512]{2,1,0:T(1,128)} %broadcast_in_dim.251), calls=%async_computation.19 | async-start | bytes 131072 | tf_op jit(solution)/shard_map/all_to_all | solution.py:17
  366.7 11.4 %all-to-all-start.20 = ((f32[32,1,512]{2,1,0:T(1,128)}), f32[32,1,512]{2,1,0:T(1,128)S(1)}, u32[]{:S(2)}, u32[]{:S(2)}) async-start(f32[32,1,512]{2,1,0:T(1,128)} %broadcast_in_dim.252), calls=%async_computation.20 | async-start | bytes 131072 | tf_op jit(solution)/shard_map/all_to_all | solution.py:17
Sparse Core Ops, SparseCore 0:
  39.8 76.2 all-gather.1
where the time goes:
time: 389 us; the launch traced here: 387 us
  waiting for transfers between devices  146 us (38%)
  blocking collectives  81.9 us (21%)
  starting transfers between devices  63.1 us (16%)
  other arithmetic  46.4 us (12%)
  matrix products  18.7 us (5%)
  between operations  15.7 us (4%)
  local copies, waits for them, and re-layouts  14.8 us (4%)
    all_to_all x7, blocking collectives, copy_for_each(): return lax.all_to_all(copies, axis, split_axis=0, concat_axis=0, tiled=True)  81.9 us
    all_gather x1, waiting for transfers between devices, body(): shard_piece = lax.all_gather(rounded_plan, 'row', axis=0, tiled=True)  76.4 us
    all_to_all x14, waiting for transfers between devices, copy_for_each(): return lax.all_to_all(copies, axis, split_axis=0, concat_axis=0, tiled=True)  69.9 us
    all_to_all x14, starting transfers between devices, copy_for_each(): return lax.all_to_all(copies, axis, split_axis=0, concat_axis=0, tiled=True)  63 us
    convert_element_type x1, other arithmetic, body(): all_one.astype(jnp.float32)[None, :]  21.3 us
    dot_general x1, matrix products, body(): jnp.dot(columns, shard_piece, preferred_element_type=jnp.float32)  17.3 us
    broadcast_in_dim x21, local copies, waits for them, and re-layouts, copy_for_each(): copies = jnp.broadcast_to(shard, (lax.axis_size(axis), *shard.shape))  9.27 us
  transfers between devices with their start and end apart: 15, of which 14 were waited for; matrix products, arithmetic and copies ran while one was open for 3% of the time, Pallas kernels for 0%

commit v1 on v0

v1 whole, which is shorter than its diff:
```python
import functools
import math

import jax
import jax.numpy as jnp
from jax import lax
from jax.experimental import pallas as pl
from jax.experimental.pallas import tpu as pltpu
from jax.sharding import PartitionSpec as P

BLOCK = 512
SWEEPS = 5
LANES = 128
TILES = BLOCK // LANES
CHUNK = 64
MESH = pl.DeviceIdType.MESH

very_low = -1e30


def copy_for_each(shard, axis):
    copies = jnp.broadcast_to(shard, (lax.axis_size(axis), *shard.shape))
    return lax.all_to_all(copies, axis, split_axis=0, concat_axis=0, tiled=True)


def in_order(blocks, dim):
    blocks = jnp.moveaxis(blocks, 0, dim)
    lengths = blocks.shape
    return blocks.reshape(*lengths[:dim], lengths[dim] * lengths[dim + 1], *lengths[dim + 2 :])


def gather_directly(shard, axis, dim):
    return in_order(copy_for_each(shard, axis), dim)


def live_slots(sizes, count):
    return (
        jnp.arange(BLOCK, dtype=jnp.int32)[None, :] < sizes[:, None]
    ).reshape(count)


def plane_neighbours():
    steps = []
    for dx in range(4):
        for dz in range(4):
            for dc in range(2):
                if dx or dz or dc:
                    far = min(dx, 4 - dx) + min(dz, 4 - dz)
                    steps.append((-far, -dc, dx, dz, dc))
    return [step[2:] for step in sorted(steps)]


def row_index(x, z, core):
    return (x * 4 + z) * 2 + core


def diagonal():
    return lax.broadcasted_iota(jnp.int32, (LANES, LANES), 0) == lax.broadcasted_iota(
        jnp.int32, (LANES, LANES), 1
    )


def sinkhorn_kernel(
    mass_scale,
    cross_ref,
    row_const_ref,
    col_const_ref,
    sizes_one_ref,
    sizes_two_ref,
    plan_ref,
    row_ref,
    col_ref,
    cost_ref,
    rho_ref,
    row_box,
    col_box,
    row_send,
    row_recv,
    col_send,
    col_recv,
):
    row = lax.axis_index("row")
    col = lax.axis_index("col")
    x, z, core = row // 8, (row // 2) % 4, row % 2
    row_peers = [lax.rem(col + step, 4) for step in (2, 1, 3)]
    col_peers = [
        row_index(lax.rem(x + dx, 4), lax.rem(z + dz, 4), lax.rem(core + dc, 2))
        for dx, dz, dc in plane_neighbours()
    ]

    barrier = pltpu.get_barrier_semaphore()
    for peer in row_peers:
        pl.semaphore_signal(barrier, inc=1, device_id=(row, peer), device_id_type=MESH)
    for peer in col_peers:
        pl.semaphore_signal(barrier, inc=1, device_id=(peer, col), device_id_type=MESH)

    total_one = jnp.float32(0)
    for block in range(sizes_one_ref.shape[0]):
        total_one = total_one + sizes_one_ref[block].astype(jnp.float32)
    total_two = jnp.float32(0)
    for block in range(sizes_two_ref.shape[0]):
        total_two = total_two + sizes_two_ref[block].astype(jnp.float32)
    log_one = jnp.log2(jnp.full((TILES, LANES), total_one, jnp.float32))
    log_two = jnp.log2(jnp.full((TILES, LANES), total_two, jnp.float32))
    size_one = sizes_one_ref[row]
    size_two = sizes_two_ref[col]
    slot = lax.broadcasted_iota(jnp.int32, (TILES, LANES), 0) * LANES + lax.broadcasted_iota(
        jnp.int32, (TILES, LANES), 1
    )
    live_row = slot < size_one
    live_col = slot < size_two

    scale = jnp.float32(2.0 / math.sqrt(mass_scale) * math.log2(math.e))
    for start in range(0, BLOCK, CHUNK):
        ids = lax.broadcasted_iota(jnp.int32, (CHUNK, BLOCK), 0) + start
        lanes = lax.broadcasted_iota(jnp.int32, (CHUNK, BLOCK), 1)
        both = (ids < size_one) & (lanes < size_two)
        rows = pl.ds(start, CHUNK)
        cost_ref[rows, :] = jnp.where(both, cross_ref[rows, :] * scale, jnp.float32(very_low))

    diag = diagonal()
    pl.semaphore_wait(barrier, 34)

    def exchange(box, mine, sweep, send, recv, targets):
        count = len(targets)
        for target in targets:
            pltpu.make_async_remote_copy(
                src_ref=box.at[sweep, mine],
                dst_ref=box.at[sweep, mine],
                send_sem=send.at[sweep],
                recv_sem=recv.at[sweep],
                device_id=target,
                device_id_type=MESH,
            ).start()
        everyone = box.at[sweep, pl.ds(0, count)]
        pltpu.make_async_copy(everyone, everyone, recv.at[sweep]).wait()
        parts = box[sweep]
        top = jnp.max(parts, axis=0)
        return top + jnp.log2(jnp.sum(jnp.exp2(parts - top[None]), axis=0))

    def sweep_body(sweep, gamma):
        for tile in range(TILES):
            column = []
            for start in range(tile * LANES, (tile + 1) * LANES, CHUNK):
                values = cost_ref[pl.ds(start, CHUNK), :] + gamma_row(gamma)
                top = jnp.max(values, axis=1, keepdims=True)
                summed = jnp.sum(jnp.exp2(values - top), axis=1, keepdims=True)
                column.append(jnp.broadcast_to(top + jnp.log2(summed), (CHUNK, LANES)))
            column = jnp.concatenate(column, axis=0)
            row_box[sweep, col, pl.ds(tile, 1), :] = jnp.sum(
                jnp.where(diag, column, 0.0), axis=0, keepdims=True
            )
        lse = exchange(
            row_box, col, sweep, row_send, row_recv, [(row, peer) for peer in row_peers]
        )
        rho = jnp.where(live_row, -log_one - lse, 0.0)
        row_ref[...] = rho
        for tile in range(TILES):
            spread = jnp.broadcast_to(rho[tile : tile + 1, :], (LANES, LANES))
            rho_ref[pl.ds(tile * LANES, LANES), :] = jnp.broadcast_to(
                jnp.sum(jnp.where(diag, spread, 0.0), axis=1, keepdims=True), (LANES, LANES)
            )
        for tile in range(TILES):
            lanes = pl.ds(tile * LANES, LANES)
            tops, sums = [], []
            for start in range(0, BLOCK, 2 * CHUNK):
                rows = pl.ds(start, 2 * CHUNK)
                values = (cost_ref[rows, lanes] + rho_ref[rows, :]).reshape(
                    2 * CHUNK // 8, 8, LANES
                )
                top = jnp.max(values, axis=0)
                tops.append(top)
                sums.append(jnp.sum(jnp.exp2(values - top[None]), axis=0))
            high = functools.reduce(jnp.maximum, tops)
            high = jnp.max(high, axis=0, keepdims=True)
            summed = sum(s * jnp.exp2(t - high) for s, t in zip(sums, tops))
            col_box[sweep, row, pl.ds(tile, 1), :] = high + jnp.log2(
                jnp.sum(summed, axis=0, keepdims=True)
            )
        lse = exchange(
            col_box, row, sweep, col_send, col_recv, [(peer, col) for peer in col_peers]
        )
        return jnp.where(live_col, -log_two - lse, 0.0)

    def gamma_row(gamma):
        return jnp.concatenate([gamma[t : t + 1, :] for t in range(TILES)], axis=1)

    gamma = lax.fori_loop(0, SWEEPS, sweep_body, jnp.zeros((TILES, LANES), jnp.float32))

    for start in range(0, BLOCK, CHUNK):
        rows = pl.ds(start, CHUNK)
        rho = rho_ref[rows, :]
        exponent = (
            cost_ref[rows, :] + jnp.concatenate([rho] * TILES, axis=1) + gamma_row(gamma)
        )
        plan_ref[rows, :] = jnp.float32(mass_scale) * jnp.exp2(exponent)
    unit = jnp.float32(math.log(2.0) / math.sqrt(mass_scale))
    row_ref[...] = jnp.where(live_row, row_ref[...] * unit + row_const_ref[...], 0.0)
    col_ref[...] = jnp.where(live_col, gamma * unit + col_const_ref[...], 0.0)

    def drain(sweep, carry):
        for box, send, count in ((row_box, row_send, 3), (col_box, col_send, 31)):
            everyone = box.at[sweep, pl.ds(0, count)]
            pltpu.make_async_copy(everyone, everyone, send.at[sweep]).wait()
        return carry

    lax.fori_loop(0, SWEEPS, drain, 0)


def sinkhorn(cross, row_const, col_const, sizes_one, sizes_two, mass_scale):
    vmem = pl.BlockSpec(memory_space=pltpu.VMEM)
    smem = pl.BlockSpec(memory_space=pltpu.SMEM)
    return pl.pallas_call(
        functools.partial(sinkhorn_kernel, mass_scale),
        out_shape=(
            jax.ShapeDtypeStruct((BLOCK, BLOCK), jnp.float32),
            jax.ShapeDtypeStruct((TILES, LANES), jnp.float32),
            jax.ShapeDtypeStruct((TILES, LANES), jnp.float32),
        ),
        in_specs=[vmem, vmem, vmem, smem, smem],
        out_specs=(vmem, vmem, vmem),
        scratch_shapes=[
            pltpu.VMEM((BLOCK, BLOCK), jnp.float32),
            pltpu.VMEM((BLOCK, LANES), jnp.float32),
            pltpu.VMEM((SWEEPS, 4, TILES, LANES), jnp.float32),
            pltpu.VMEM((SWEEPS, 32, TILES, LANES), jnp.float32),
            pltpu.SemaphoreType.DMA((SWEEPS,)),
            pltpu.SemaphoreType.DMA((SWEEPS,)),
            pltpu.SemaphoreType.DMA((SWEEPS,)),
            pltpu.SemaphoreType.DMA((SWEEPS,)),
        ],
        compiler_params=pltpu.CompilerParams(collective_id=0, has_side_effects=True),
        name="sinkhorn",
    )(cross, row_const, col_const, sizes_one, sizes_two)


def body(graph_one, graph_two, coupling, sizes_one, sizes_two):
    local_rows = graph_one.shape[0]
    count_one = graph_one.shape[1]
    local_cols = graph_two.shape[0]
    count_two = graph_two.shape[1]
    all_one = live_slots(sizes_one, count_one)
    all_two = live_slots(sizes_two, count_two)
    slots = jnp.arange(BLOCK, dtype=jnp.int32)
    live_rows = slots < sizes_one[lax.axis_index("row")]
    live_cols = slots < sizes_two[lax.axis_index("col")]
    total_one = jnp.sum(sizes_one).astype(jnp.float32)
    total_two = jnp.sum(sizes_two).astype(jnp.float32)
    live_both = live_rows[:, None] & live_cols[None, :]
    rounded_plan = jnp.where(live_both, coupling, jnp.float32(0.0)).astype(jnp.bfloat16)
    whole_plan = lax.all_gather(rounded_plan, "row", axis=0, tiled=True)
    first_product = jnp.dot(graph_one, whole_plan, preferred_element_type=jnp.float32).astype(
        jnp.bfloat16
    )
    whole_first = gather_directly(first_product, "col", 1)
    cross_term = lax.dot_general(
        whole_first, graph_two, (((1,), (1,)), ((), ())), preferred_element_type=jnp.float32
    )
    row_const = (
        jnp.sum(
            jnp.square(graph_one.astype(jnp.float32)) * all_one.astype(jnp.float32)[None, :], axis=1
        )
        / total_one
    )
    col_const = (
        jnp.sum(
            jnp.square(graph_two.astype(jnp.float32)) * all_two.astype(jnp.float32)[None, :], axis=1
        )
        / total_two
    )
    plan, row_potential, col_potential = sinkhorn(
        cross_term,
        row_const.reshape(TILES, LANES),
        col_const.reshape(TILES, LANES),
        sizes_one,
        sizes_two,
        float(count_one * count_two),
    )
    return plan, row_potential.reshape(local_rows), col_potential.reshape(local_cols)


def solution(mesh):
    return jax.shard_map(
        body,
        mesh=mesh,
        in_specs=(P("row", None), P("col", None), P("row", "col"), P(), P()),
        out_specs=(P("row", "col"), P("row"), P("col")),
        check_vma=False,
    )
```

time: 389 us -> 205 us (0.53)
  blocking collectives: 81.9 us -> 0 us
  starting transfers between devices: 63.1 us -> 4.48 us
  waiting for transfers between devices: 146 us -> 88.7 us
  Pallas kernels: 0 us -> 49.7 us
  other arithmetic: 46.4 us -> 16.1 us
  local copies, waits for them, and re-layouts: 14.8 us -> 8.75 us
    all_to_all x7 -> x0, blocking collectives: 81.9 us -> none  [copy_for_each(): return lax.all_to_all(copies, axis, split_axis=0, concat_axis=0, tiled=True)]
    all_to_all x14 -> x1, starting transfers between devices: 63 us -> 4.44 us  [copy_for_each(): return lax.all_to_all(copies, axis, split_axis=0, concat_axis=0, tiled=True)]
    all_to_all x14 -> x1, waiting for transfers between devices: 69.9 us -> 15.2 us  [copy_for_each(): return lax.all_to_all(copies, axis, split_axis=0, concat_axis=0, tiled=True)]
    pallas_call x0 -> x1, Pallas kernels: none -> 49.7 us  [sinkhorn(): pl.pallas_call(functools.partial(sinkhorn_kernel, mass_scale), out_shape=...]
    convert_element_type x2 -> x0, other arithmetic: 24.6 us -> none  [the longest x1 21.3 us: body(): all_one.astype(jnp.float32)[None, :]]
    broadcast_in_dim x21 -> x1, local copies, waits for them, and re-layouts: 9.27 us -> 1.46 us  [copy_for_each(): copies = jnp.broadcast_to(shard, (lax.axis_size(axis), *shard.shape))]
    gather x3 -> x0, local copies, waits for them, and re-layouts: 5.39 us -> none  [live_slots(): jnp.repeat(sizes, BLOCK, total_repeat_length=count)]
    unnamed x6 -> x11, local copies, waits for them, and re-layouts: 0.01 us -> 4.81 us
  transfers between devices with their start and end apart: 15 -> 2, of which waited for: 14 -> 2; matrix products, arithmetic and copies ran while one was open for 3% -> 6% of each run, Pallas kernels for 0% -> 0%
where the time goes in v1:
time: 205 us; the launch traced here: 204 us
  waiting for transfers between devices  88.7 us (43%)
  Pallas kernels  49.7 us (24%)
  matrix products  21.1 us (10%)
  other arithmetic  16.1 us (8%)
  between operations  15.4 us (8%)
  local copies, waits for them, and re-layouts  8.75 us (4%)
  starting transfers between devices  4.48 us (2%)
    all_gather x1, waiting for transfers between devices, body(): whole_plan = lax.all_gather(rounded_plan, 'row', axis=0, tiled=True)  73.5 us
    pallas_call x1, Pallas kernels, sinkhorn(): pl.pallas_call(functools.partial(sinkhorn_kernel, mass_scale), out_shape=...  49.7 us
    dot_general x1, matrix products, body(): jnp.dot(graph_one, whole_plan, preferred_element_type=jnp.float32)  17.2 us
    all_to_all x1, waiting for transfers between devices, copy_for_each(): return lax.all_to_all(copies, axis, split_axis=0, concat_axis=0, tiled=True)  15.2 us
    reduce_sum x1, other arithmetic, body(): jnp.sum(jnp.square(graph_one.astype(jnp.float32)) * all_one.astype(jnp.fl...  7.76 us
    unnamed x11, local copies, waits for them, and re-layouts  4.81 us
    all_to_all x1, starting transfers between devices, copy_for_each(): return lax.all_to_all(copies, axis, split_axis=0, concat_axis=0, tiled=True)  4.44 us
  transfers between devices with their start and end apart: 2, of which 2 were waited for; matrix products, arithmetic and copies ran while one was open for 6% of the time, Pallas kernels for 0%

profile of v1, /device:TPU:1, one launch (start us, length us, event | category | flops | bytes accessed | tf_op | source)
XLA Modules:
  0.0 204.3 jit_solution(18325789345944567090)
XLA Ops:
  7.2 0.0 all-gather.2.cloned.1.call-start
  7.2 1.2 dynamic_slice.6
  8.5 1.2 dynamic_slice.7
  9.7 1.3 iota_compare_fusion.2
  11.0 2.2 %select_convert_fusion = bf16[512,512]{1,0:T(8,128)(2,1)} fusion(f32[512,512]{1,0:T(8,128)} %param.7, pred[512]{0:T(512)(128)(4,1)S(1)} %get-tuple-element.9, pred[512]{0:T(512)(128)(4,1)S(1)} %get-tuple-element.10), kind=kLoop, calls=%fused_computation.4 | loop fusion | flops 524288 | bytes 1573888 | tf_op jit(solution)/shard_map/convert_element_type | solution.py:250
  13.2 0.0 all-gather.2.cloned.1.call-update
  13.2 0.7 convert_bitcast_fusion.1
  14.0 2.2 %multiply_reduce_fusion.1 = f32[512]{0:T(512)S(1)} fusion(bf16[512,2048]{1,0:T(8,128)(2,1)} %param.6, f32[2048]{0:T(1024)S(1)} %bitcast.24), kind=kLoop, calls=%fused_computation.1 | loop fusion | flops 4193792 | bytes 2107392 | tf_op jit(solution)/shard_map/reduce_sum | solution.py:266
  16.2 73.5 %all-gather.2.cloned.1.call-done = bf16[16384,512]{1,0:T(8,128)(2,1)} async-done(((bf16[512,512]{1,0:T(8,128)(2,1)}), bf16[16384,512]{1,0:T(8,128)(2,1)}) %all-gather.2.cloned.1.call-update) | async-done | bytes 16777232 | tf_op jit(solution)/shard_map/all_gather | solution.py:251
  89.7 17.2 %fusion = bf16[512,512]{0,1:T(8,128)(2,1)S(1)} fusion(bf16[16384,512]{1,0:T(8,128)(2,1)} %all-gather.2.cloned.1.call-done, bf16[512,16384]{1,0:T(8,128)(2,1)} %param.5), kind=kOutput, calls=%fused_computation.3 | convolution fusion | flops 8590196736 | bytes 34078720 | tf_op jit(solution)/shard_map/dot_general | solution.py:252
  106.9 0.0 copy-start.1
  106.9 1.5 broadcast_in_dim.6
  108.4 4.4 %all-to-all-start = ((bf16[4,512,512]{1,2,0:T(8,128)(2,1)}), bf16[4,512,512]{1,2,0:T(8,128)(2,1)}, u32[]{:S(2)}, u32[]{:S(2)}) async-start(bf16[4,512,512]{1,2,0:T(8,128)(2,1)} %broadcast_in_dim.6), calls=%async_computation | async-start | bytes 4194304 | tf_op jit(solution)/shard_map/all_to_all | solution.py:23
  112.9 0.1 convert_bitcast_fusion
  112.9 0.6 reduce_sum.37
  113.6 0.6 reduce_sum.39
  115.5 7.8 %multiply_reduce_fusion = f32[512]{0:T(512)S(1)} fusion(bf16[512,16384]{1,0:T(8,128)(2,1)} %param.5, f32[16384]{0:T(1024)S(1)} %bitcast.23), kind=kLoop, calls=%fused_computation | loop fusion | flops 33553920 | bytes 16844800 | tf_op jit(solution)/shard_map/reduce_sum | solution.py:260
  123.3 0.6 divide_bitcast_fusion
  123.9 15.2 %all-to-all-done = bf16[4,512,512]{1,2,0:T(8,128)(2,1)} async-done(((bf16[4,512,512]{1,2,0:T(8,128)(2,1)}), bf16[4,512,512]{1,2,0:T(8,128)(2,1)}, u32[]{:S(2)}, u32[]{:S(2)}) %all-to-all-start) | async-done | bytes 2097184 | tf_op jit(solution)/shard_map/all_to_all | solution.py:23
  139.1 3.9 %fusion.1.cross_ref = f32[512,512]{1,0:T(8,128)} fusion(bf16[512,2048]{0,1:T(8,128)(2,1)} %bitcast.4, bf16[512,2048]{1,0:T(8,128)(2,1)S(1)} %copy-done), kind=kOutput, calls=%fused_computation.13 | convolution fusion | flops 1073741824 | bytes 5242880 | tf_op jit(solution)/shard_map/dot_general | solution.py:256
  143.0 49.7 %sinkhorn.1 = (f32[512,512]{1,0:T(8,128)}, f32[4,128]{1,0:T(4,128)}, f32[4,128]{1,0:T(4,128)}) custom-call(f32[512,512]{1,0:T(8,128)} %fusion.1.cross_ref, f32[4,128]{1,0:T(4,128)} %get-tuple-element.12.row_const_ref, f32[4,128]{1,0:T(4,128)} %get-tuple-element.11.col_const_ref, s32[32]{0:T(128)} %sizes_one_ref.1, s32[4]{0:T(128)} %sizes_two_ref.1), custom_call_target="tpu_custom_call" | custom-call | tf_op jit(solution)/shard_map/sinkhorn/pallas_call | solution.py:213
  192.7 2.3 %copy.14 = f32[512,512]{1,0:T(8,128)} copy(f32[512,512]{1,0:T(8,128)} %get-tuple-element.16) | data formatting | bytes 2097152
  194.9 1.3 copy.15
  196.2 1.3 copy.16
  (7 shorter events, 0.0 us)
Async XLA Ops:
  7.2 82.5 %all-gather.2.cloned.1.call-start = ((), (), s32[]{:S(2)}) async-start(), calls=%async_computation.1 | async-start | bytes 17301504 | tf_op jit(solution)/shard_map/all_gather | solution.py:251
  106.9 5.9 %copy-start.1 = (s32[32]{0:T(128)S(1)}, s32[32]{0:T(128)}, u32[]{:S(2)}) copy-start(s32[32]{0:T(128)} %sizes_one_ref.1) | copy-start | bytes 388
  106.9 6.6 %copy-start.2 = (s32[4]{0:T(128)S(1)}, s32[4]{0:T(128)}, u32[]{:S(2)}) copy-start(s32[4]{0:T(128)} %sizes_two_ref.1) | copy-start | bytes 52
  108.4 30.7 %all-to-all-start = ((bf16[4,512,512]{1,2,0:T(8,128)(2,1)}), bf16[4,512,512]{1,2,0:T(8,128)(2,1)}, u32[]{:S(2)}, u32[]{:S(2)}) async-start(bf16[4,512,512]{1,2,0:T(8,128)(2,1)} %broadcast_in_dim.6), calls=%async_computation | async-start | bytes 4194304 | tf_op jit(solution)/shard_map/all_to_all | solution.py:23
  115.5 23.6 %copy-start = (bf16[512,2048]{1,0:T(8,128)(2,1)S(1)}, bf16[512,2048]{1,0:T(8,128)(2,1)}, u32[]{:S(2)}) copy-start(bf16[512,2048]{1,0:T(8,128)(2,1)} %param.6) | copy-start | bytes 6291460
Sparse Core Ops, SparseCore 0:
  13.4 76.2 all-gather.1

commit v2 on v1

v2 whole, which is shorter than its diff:
```python
import functools
import math

import jax
import jax.numpy as jnp
from jax import lax
from jax.experimental import pallas as pl
from jax.experimental.pallas import tpu as pltpu
from jax.sharding import PartitionSpec as P

BLOCK = 512
SWEEPS = 5
LANES = 128
TILES = BLOCK // LANES
CHUNK = 64
WIDTHS = (256, 256)
STEPS = (
    (0, 0), (-1, 0), (1, 0), (0, -1), (0, 1), (2, 0), (-1, -1), (-1, 1),
    (1, -1), (1, 1), (0, 2), (2, -1), (2, 1), (-1, 2), (1, 2), (2, 2),
)
HALF = BLOCK // 2
UNIT = BLOCK // 4
MESH = pl.DeviceIdType.MESH

very_low = -1e30


def plane_neighbours():
    steps = []
    for dx in range(4):
        for dz in range(4):
            for dc in range(2):
                if dx or dz or dc:
                    far = min(dx, 4 - dx) + min(dz, 4 - dz)
                    steps.append((-far, -dc, dx, dz, dc))
    return [step[2:] for step in sorted(steps)]


def row_index(x, z, core):
    return (x * 4 + z) * 2 + core


def diagonal():
    return lax.broadcasted_iota(jnp.int32, (LANES, LANES), 0) == lax.broadcasted_iota(
        jnp.int32, (LANES, LANES), 1
    )


def gw_kernel(
    mass_scale,
    graph_one_ref,
    graph_two_ref,
    coupling_ref,
    sizes_one_ref,
    sizes_two_ref,
    cost_ref,
    rho_ref,
    vectors_ref,
    *scratch,
):
    parts = len(WIDTHS)
    plans, scratch = scratch[:parts], scratch[parts:]
    firsts, scratch = scratch[:parts], scratch[parts:]
    totals, scratch = scratch[:parts], scratch[parts:]
    (
        one_ref,
        two_ref,
        loaded_ref,
        squares_ref,
        row_box,
        col_box,
        load_sem,
        plan_send,
        plan_recv,
        pair_recv,
        first_send,
        first_recv,
        row_send,
        row_recv,
        col_send,
        col_recv,
    ) = scratch
    row = lax.axis_index("row")
    col = lax.axis_index("col")
    x, z, core = row // 8, (row // 2) % 4, row % 2
    partner = row + 1 - 2 * core
    row_peers = [lax.rem(col + step, 4) for step in (2, 1, 3)]
    col_peers = [
        row_index(lax.rem(x + dx, 4), lax.rem(z + dz, 4), lax.rem(core + dc, 2))
        for dx, dz, dc in plane_neighbours()
    ]

    barrier = pltpu.get_barrier_semaphore()
    for peer in row_peers:
        pl.semaphore_signal(barrier, inc=1, device_id=(row, peer), device_id_type=MESH)
    for peer in col_peers:
        pl.semaphore_signal(barrier, inc=1, device_id=(peer, col), device_id_type=MESH)

    load_coupling = pltpu.make_async_copy(coupling_ref, loaded_ref, load_sem.at[0])
    load_coupling.start()
    load_two = []
    for block in range(4):
        load_two.append(
            pltpu.make_async_copy(
                graph_two_ref.at[:, pl.ds(block * BLOCK, BLOCK)], two_ref.at[block], load_sem.at[1]
            )
        )
    load_one = []
    for block in range(32):
        load_one.append(
            pltpu.make_async_copy(
                graph_one_ref.at[:, pl.ds(block * BLOCK, BLOCK)], one_ref.at[block], load_sem.at[2]
            )
        )

    total_one = jnp.float32(0)
    for block in range(sizes_one_ref.shape[0]):
        total_one = total_one + sizes_one_ref[block].astype(jnp.float32)
    total_two = jnp.float32(0)
    for block in range(sizes_two_ref.shape[0]):
        total_two = total_two + sizes_two_ref[block].astype(jnp.float32)
    all_one = jnp.full((TILES, LANES), total_one, jnp.float32)
    all_two = jnp.full((TILES, LANES), total_two, jnp.float32)
    log_one = jnp.log2(all_one)
    log_two = jnp.log2(all_two)
    size_one = sizes_one_ref[row]
    size_two = sizes_two_ref[col]
    slot = lax.broadcasted_iota(jnp.int32, (TILES, LANES), 0) * LANES + lax.broadcasted_iota(
        jnp.int32, (TILES, LANES), 1
    )
    live_row = slot < size_one
    live_col = slot < size_two
    diag = diagonal()

    def live_part(start, width, offset=0):
        ids = lax.broadcasted_iota(jnp.int32, (CHUNK, width), 0) + start
        lanes = lax.broadcasted_iota(jnp.int32, (CHUNK, width), 1) + offset
        return (ids < size_one) & (lanes < size_two)

    load_coupling.wait()
    for copy in load_two + load_one:
        copy.start()
    for start in range(0, BLOCK, CHUNK):
        rows = pl.ds(start, CHUNK)
        offset = 0
        for part, width in enumerate(WIDTHS):
            kept = jnp.where(
                live_part(start, width, offset), loaded_ref[rows, pl.ds(offset, width)], 0.0
            )
            plans[part][row, rows, :] = kept.astype(jnp.bfloat16)
            offset += width
    squares_ref[...] = jnp.zeros_like(squares_ref)
    pl.semaphore_wait(barrier, 34)

    def place(half, first, second):
        dx, dz = (first, second) if half == 0 else (second, first)
        return row_index(lax.rem(x + dx + 4, 4), lax.rem(z + dz + 4, 4), core)

    def send_unit(part, step, half, turn, source, target):
        rows = pl.ds(half * HALF + turn * UNIT, UNIT)
        piece = plans[part].at[source, rows, :]
        pltpu.make_async_remote_copy(
            src_ref=piece,
            dst_ref=piece,
            send_sem=plan_send.at[part],
            recv_sem=plan_recv.at[part, step, half, turn],
            device_id=(target, col),
            device_id_type=MESH,
        ).start()

    def send_pair(part, step, half, source):
        piece = plans[part].at[source, pl.ds(half * HALF, HALF), :]
        pltpu.make_async_remote_copy(
            src_ref=piece,
            dst_ref=piece,
            send_sem=plan_send.at[part],
            recv_sem=pair_recv.at[part, step],
            device_id=(partner, col),
            device_id_type=MESH,
        ).start()

    def wait_bytes(ref, sem):
        pltpu.make_async_copy(ref, ref, sem).wait()

    def moves(part, step):
        first, second = STEPS[step]
        for half in range(2):
            source = place(half, first, second)
            for turn in range(2):
                if (first, second) != (0, 0):
                    rows = pl.ds(half * HALF + turn * UNIT, UNIT)
                    wait_bytes(
                        plans[part].at[source, rows, :], plan_recv.at[part, step, half, turn]
                    )
                onward = -1 if turn == 0 else 1
                if second == 0:
                    for sent in (-1, 1):
                        if first == 0 or (first == onward and sent == onward):
                            seen = sent if first == 0 else 2
                            send_unit(
                                part, STEPS.index((seen, 0)), half, turn, source,
                                place(half, -sent, 0),
                            )
                    for sent in (-1, 1):
                        send_unit(
                            part, STEPS.index((first, sent)), half, turn, source,
                            place(half, 0, -sent),
                        )
                elif second == onward:
                    send_unit(
                        part, STEPS.index((first, 2)), half, turn, source, place(half, 0, -onward)
                    )
            send_pair(part, step, half, source)

    def offset_of(step, axis):
        value = jnp.int32(STEPS[-1][axis])
        for index in range(len(STEPS) - 1):
            value = jnp.where(step == index, jnp.int32(STEPS[index][axis]), value)
        return value

    def multiply(part, step, parity):
        first, second = offset_of(step, 0), offset_of(step, 1)
        for half in range(2):
            source = place(half, first, second)
            source = source + parity * (1 - 2 * core)
            rows = pl.ds(half * HALF, HALF)
            left = one_ref[source, :, rows]
            totals[part][...] += jnp.dot(
                left, plans[part][source, rows, :], preferred_element_type=jnp.float32
            )
            if part == 0:
                size = sizes_one_ref[source]
                for start in range(0, BLOCK, CHUNK):
                    squares = squares_ref[pl.ds(start, CHUNK), :]
                    for tile in range(2):
                        lanes = half * HALF + tile * LANES
                        ids = lax.broadcasted_iota(jnp.int32, (CHUNK, LANES), 1) + lanes
                        value = one_ref[source, pl.ds(start, CHUNK), pl.ds(lanes, LANES)].astype(
                            jnp.float32
                        )
                        squares = squares + jnp.where(ids < size, value * value, 0.0)
                    squares_ref[pl.ds(start, CHUNK), :] = squares

    def first_copy(part, half, source, key, target):
        piece = firsts[part].at[source, pl.ds(half * HALF, HALF), :]
        return pltpu.make_async_remote_copy(
            src_ref=piece,
            dst_ref=piece,
            send_sem=first_send.at[part],
            recv_sem=first_recv.at[part, key],
            device_id=(row, target),
            device_id_type=MESH,
        )

    up, down, across = lax.rem(col + 1, 4), lax.rem(col + 3, 4), lax.rem(col + 2, 4)

    def first_start(part):
        for start in range(0, BLOCK, CHUNK):
            rows = pl.ds(start, CHUNK)
            firsts[part][col, rows, :] = totals[part][rows, :].astype(jnp.bfloat16)
        first_copy(part, 0, col, 0, up).start()
        first_copy(part, 1, col, 1, down).start()
        first_copy(part, 1, col, 2, up).start()
        first_copy(part, 0, col, 3, down).start()

    def first_wait(part, half, source, key):
        wait_bytes(firsts[part].at[source, pl.ds(half * HALF, HALF), :], first_recv.at[part, key])

    def first_onward(part):
        first_wait(part, 0, down, 0)
        first_copy(part, 0, down, 4, up).start()
        first_wait(part, 1, up, 1)
        first_copy(part, 1, up, 5, down).start()

    def cross_add(part, source, fresh=False):
        offset = sum(WIDTHS[:part])
        added = lax.dot_general(
            firsts[part][source],
            two_ref[source, :, pl.ds(offset, WIDTHS[part])],
            (((1,), (1,)), ((), ())),
            preferred_element_type=jnp.float32,
        )
        if fresh:
            cost_ref[...] = added
        else:
            cost_ref[...] += added

    def first_end(part):
        cross_add(part, col, fresh=part == 0)
        first_wait(part, 1, down, 2)
        cross_add(part, down)
        first_wait(part, 0, up, 3)
        cross_add(part, up)
        first_wait(part, 0, across, 4)
        first_wait(part, 1, across, 5)
        cross_add(part, across)

    last = len(STEPS) - 1
    for part in range(parts):
        totals[part][...] = jnp.zeros_like(totals[part])
    moves(0, 0)
    if parts > 1:
        moves(1, 0)
    wait_bytes(two_ref, load_sem.at[1])
    col_square = []
    for tile in range(TILES):
        summed = []
        for start in range(tile * LANES, (tile + 1) * LANES, CHUNK):
            gathered = jnp.zeros((CHUNK, LANES), jnp.float32)
            for block in range(4):
                for lane in range(TILES):
                    ids = lax.broadcasted_iota(jnp.int32, (CHUNK, LANES), 1) + lane * LANES
                    value = two_ref[block, pl.ds(start, CHUNK), pl.ds(lane * LANES, LANES)].astype(
                        jnp.float32
                    )
                    gathered = gathered + jnp.where(
                        ids < sizes_two_ref[block], value * value, 0.0
                    )
            summed.append(
                jnp.broadcast_to(jnp.sum(gathered, axis=1, keepdims=True), (CHUNK, LANES))
            )
        vectors_ref[pl.ds(12 + tile, 1), :] = jnp.sum(
            jnp.where(diag, jnp.concatenate(summed, axis=0), 0.0), axis=0, keepdims=True
        )
    wait_bytes(one_ref, load_sem.at[2])

    for part in range(parts):

        def one_step(step, carry, part=part):
            for index in range(1, len(STEPS)):

                @pl.when(step == index)
                def _():
                    moves(part, index)
                    if index == 6 and 1 < part + 1 < parts:
                        moves(part + 1, 0)
                    if part and index == 5:
                        first_onward(part - 1)
                    if part and index == 11:
                        first_end(part - 1)

            multiply(part, step, 0)

            @pl.when(step > 0)
            def _():
                wait_bytes(plans[part].at[0], pair_recv.at[part, lax.max(step - 1, 0)])
                multiply(part, lax.max(step - 1, 0), 1)

            return carry

        lax.fori_loop(0, len(STEPS), one_step, 0)
        wait_bytes(plans[part].at[0], pair_recv.at[part, last])
        multiply(part, last, 1)
        first_start(part)
    first_onward(parts - 1)
    for tile in range(TILES):
        column = jnp.broadcast_to(
            jnp.sum(squares_ref[pl.ds(tile * LANES, LANES), :], axis=1, keepdims=True),
            (LANES, LANES),
        )
        vectors_ref[pl.ds(8 + tile, 1), :] = jnp.sum(
            jnp.where(diag, column, 0.0), axis=0, keepdims=True
        )
    first_end(parts - 1)

    scale = jnp.float32(2.0 / math.sqrt(mass_scale) * math.log2(math.e))
    for start in range(0, BLOCK, CHUNK):
        rows = pl.ds(start, CHUNK)
        cost_ref[rows, :] = jnp.where(
            live_part(start, BLOCK), cost_ref[rows, :] * scale, jnp.float32(very_low)
        )

    def exchange(box, mine, sweep, send, recv, targets):
        for target in targets:
            pltpu.make_async_remote_copy(
                src_ref=box.at[sweep, mine],
                dst_ref=box.at[sweep, mine],
                send_sem=send.at[sweep],
                recv_sem=recv.at[sweep],
                device_id=target,
                device_id_type=MESH,
            ).start()
        wait_bytes(box.at[sweep, pl.ds(0, len(targets))], recv.at[sweep])
        logs = box[sweep]
        top = jnp.max(logs, axis=0)
        return top + jnp.log2(jnp.sum(jnp.exp2(logs - top[None]), axis=0))

    def gamma_row(gamma):
        return jnp.concatenate([gamma[t : t + 1, :] for t in range(TILES)], axis=1)

    def sweep_body(sweep, gamma):
        for tile in range(TILES):
            column = []
            for start in range(tile * LANES, (tile + 1) * LANES, CHUNK):
                values = cost_ref[pl.ds(start, CHUNK), :] + gamma_row(gamma)
                top = jnp.max(values, axis=1, keepdims=True)
                summed = jnp.sum(jnp.exp2(values - top), axis=1, keepdims=True)
                column.append(jnp.broadcast_to(top + jnp.log2(summed), (CHUNK, LANES)))
            column = jnp.concatenate(column, axis=0)
            row_box[sweep, col, pl.ds(tile, 1), :] = jnp.sum(
                jnp.where(diag, column, 0.0), axis=0, keepdims=True
            )
        lse = exchange(
            row_box, col, sweep, row_send, row_recv, [(row, peer) for peer in row_peers]
        )
        rho = jnp.where(live_row, -log_one - lse, 0.0)
        vectors_ref[pl.ds(0, TILES), :] = rho
        for tile in range(TILES):
            spread = jnp.broadcast_to(rho[tile : tile + 1, :], (LANES, LANES))
            rho_ref[pl.ds(tile * LANES, LANES), :] = jnp.broadcast_to(
                jnp.sum(jnp.where(diag, spread, 0.0), axis=1, keepdims=True), (LANES, LANES)
            )
        for tile in range(TILES):
            lanes = pl.ds(tile * LANES, LANES)
            tops, sums = [], []
            for start in range(0, BLOCK, 2 * CHUNK):
                rows = pl.ds(start, 2 * CHUNK)
                values = (cost_ref[rows, lanes] + rho_ref[rows, :]).reshape(
                    2 * CHUNK // 8, 8, LANES
                )
                top = jnp.max(values, axis=0)
                tops.append(top)
                sums.append(jnp.sum(jnp.exp2(values - top[None]), axis=0))
            high = functools.reduce(jnp.maximum, tops)
            high = jnp.max(high, axis=0, keepdims=True)
            summed = sum(s * jnp.exp2(t - high) for s, t in zip(sums, tops))
            col_box[sweep, row, pl.ds(tile, 1), :] = high + jnp.log2(
                jnp.sum(summed, axis=0, keepdims=True)
            )
        lse = exchange(
            col_box, row, sweep, col_send, col_recv, [(peer, col) for peer in col_peers]
        )
        return jnp.where(live_col, -log_two - lse, 0.0)

    gamma = lax.fori_loop(0, SWEEPS, sweep_body, jnp.zeros((TILES, LANES), jnp.float32))

    unit = jnp.float32(math.log(2.0) / math.sqrt(mass_scale))
    rho = vectors_ref[pl.ds(0, TILES), :]
    row_const = vectors_ref[pl.ds(8, TILES), :] / all_one
    col_const = vectors_ref[pl.ds(12, TILES), :] / all_two
    vectors_ref[pl.ds(4, TILES), :] = gamma
    vectors_ref[pl.ds(8, TILES), :] = jnp.where(live_row, rho * unit + row_const, 0.0)
    vectors_ref[pl.ds(12, TILES), :] = jnp.where(live_col, gamma * unit + col_const, 0.0)

    def drain(sweep, carry):
        for box, send, count in ((row_box, row_send, 3), (col_box, col_send, 31)):
            wait_bytes(box.at[sweep, pl.ds(0, count)], send.at[sweep])
        return carry

    lax.fori_loop(0, SWEEPS, drain, 0)
    for part in range(parts):
        wait_bytes(plans[part].at[pl.ds(0, 31)], plan_send.at[part])
        wait_bytes(firsts[part].at[pl.ds(0, 3)], first_send.at[part])


def finish_kernel(mass_scale, cost_ref, rho_ref, vectors_ref, plan_ref, row_ref, col_ref):
    gamma = jnp.concatenate([vectors_ref[pl.ds(4 + t, 1), :] for t in range(TILES)], axis=1)
    for start in range(0, BLOCK, CHUNK):
        rows = pl.ds(start, CHUNK)
        exponent = (
            cost_ref[rows, :] + jnp.concatenate([rho_ref[rows, :]] * TILES, axis=1) + gamma
        )
        plan_ref[rows, :] = jnp.float32(mass_scale) * jnp.exp2(exponent)
    row_ref[...] = vectors_ref[pl.ds(8, TILES), :]
    col_ref[...] = vectors_ref[pl.ds(12, TILES), :]


def body(graph_one, graph_two, coupling, sizes_one, sizes_two):
    mass_scale = float(graph_one.shape[1] * graph_two.shape[1])
    vmem = pl.BlockSpec(memory_space=pltpu.VMEM)
    smem = pl.BlockSpec(memory_space=pltpu.SMEM)
    hbm = pl.BlockSpec(memory_space=pltpu.HBM)
    parts = len(WIDTHS)
    f32, bf16 = jnp.float32, jnp.bfloat16
    dma = pltpu.SemaphoreType.DMA
    cost, rho, vectors = pl.pallas_call(
        functools.partial(gw_kernel, mass_scale),
        out_shape=(
            jax.ShapeDtypeStruct((BLOCK, BLOCK), f32),
            jax.ShapeDtypeStruct((BLOCK, LANES), f32),
            jax.ShapeDtypeStruct((4 * TILES, LANES), f32),
        ),
        in_specs=[hbm, hbm, hbm, smem, smem],
        out_specs=(vmem, vmem, vmem),
        scratch_shapes=[
            *(pltpu.VMEM((32, BLOCK, width), bf16) for width in WIDTHS),
            *(pltpu.VMEM((4, BLOCK, width), bf16) for width in WIDTHS),
            *(pltpu.VMEM((BLOCK, width), f32) for width in WIDTHS),
            pltpu.VMEM((32, BLOCK, BLOCK), bf16),
            pltpu.VMEM((4, BLOCK, BLOCK), bf16),
            pltpu.VMEM((BLOCK, BLOCK), f32),
            pltpu.VMEM((BLOCK, LANES), f32),
            pltpu.VMEM((SWEEPS, 4, TILES, LANES), f32),
            pltpu.VMEM((SWEEPS, 32, TILES, LANES), f32),
            dma((3,)),
            dma((parts,)),
            dma((parts, len(STEPS), 2, 2)),
            dma((parts, len(STEPS))),
            dma((parts,)),
            dma((parts, 6)),
            dma((SWEEPS,)),
            dma((SWEEPS,)),
            dma((SWEEPS,)),
            dma((SWEEPS,)),
        ],
        compiler_params=pltpu.CompilerParams(
            collective_id=0, has_side_effects=True, vmem_limit_bytes=56 * 1024 * 1024
        ),
        name="gw_step",
    )(graph_one, graph_two, coupling, sizes_one, sizes_two)
    plan, row_potential, col_potential = pl.pallas_call(
        functools.partial(finish_kernel, mass_scale),
        out_shape=(
            jax.ShapeDtypeStruct((BLOCK, BLOCK), f32),
            jax.ShapeDtypeStruct((TILES, LANES), f32),
            jax.ShapeDtypeStruct((TILES, LANES), f32),
        ),
        in_specs=[vmem, vmem, vmem],
        out_specs=(vmem, vmem, vmem),
        name="finish",
    )(cost, rho, vectors)
    return plan, row_potential.reshape(BLOCK), col_potential.reshape(BLOCK)


def solution(mesh):
    return jax.shard_map(
        body,
        mesh=mesh,
        in_specs=(P("row", None), P("col", None), P("row", "col"), P(), P()),
        out_specs=(P("row", "col"), P("row"), P("col")),
        check_vma=False,
    )
```

time: 205 us -> 128 us (0.62)
  waiting for transfers between devices: 88.7 us -> 0 us
  Pallas kernels: 49.7 us -> 127 us
  matrix products: 21.1 us -> 0 us
  other arithmetic: 16.1 us -> 0 us
  between operations: 15.4 us -> 0.64 us
  local copies, waits for them, and re-layouts: 8.75 us -> 0 us
  starting transfers between devices: 4.48 us -> 0 us
    pallas_call x1 -> x2, Pallas kernels: 49.7 us -> 127 us  [the longest x1 125 us: body(): pl.pallas_call(functools.partial(gw_kernel, mass_scale), out_shape=(jax.S...]
    all_gather x1 -> x0, waiting for transfers between devices: 73.5 us -> none  [body(): whole_plan = lax.all_gather(rounded_plan, 'row', axis=0, tiled=True)]
    dot_general x2 -> x0, matrix products: 21.1 us -> none  [the longest x1 17.2 us: body(): jnp.dot(graph_one, whole_plan, preferred_element_type=jnp.float32)]
    all_to_all x1 -> x0, waiting for transfers between devices: 15.2 us -> none  [copy_for_each(): return lax.all_to_all(copies, axis, split_axis=0, concat_axis=0, tiled=True)]
    reduce_sum x4 -> x0, other arithmetic: 11.2 us -> none  [the longest x1 7.76 us: body(): jnp.sum(jnp.square(graph_one.astype(jnp.float32)) * all_one.astype(jnp.fl...]
    unnamed x11 -> x0, local copies, waits for them, and re-layouts: 4.81 us -> none
    all_to_all x1 -> x0, starting transfers between devices: 4.44 us -> none  [copy_for_each(): return lax.all_to_all(copies, axis, split_axis=0, concat_axis=0, tiled=True)]
    dynamic_slice x2 -> x0, local copies, waits for them, and re-layouts: 2.48 us -> none  [the longest x1 1.24 us: body(): live_rows = slots < sizes_one[lax.axis_index('row')]]
  transfers between devices with their start and end apart: 2 -> 0, of which waited for: 2 -> 0; matrix products, arithmetic and copies ran while one was open for 6% -> 0% of each run, Pallas kernels for 0% -> 0%
where the time goes in v2:
time: 128 us
  Pallas kernels  127 us (99%)
    pallas_call x1, Pallas kernels, body(): pl.pallas_call(functools.partial(gw_kernel, mass_scale), out_shape=(jax.S...  125 us

profile of v2, /device:TPU:1, one launch (start us, length us, event | category | flops | bytes accessed | tf_op | source)
XLA Modules:
  0.0 127.9 jit_solution(2146832891506979406)
XLA Ops:
  0.6 124.9 %gw_step.1 = (f32[512,512]{1,0:T(8,128)}, f32[512,128]{1,0:T(8,128)}, f32[16,128]{1,0:T(8,128)}) custom-call(bf16[512,16384]{1,0:T(8,128)(2,1)} %graph_one_ref.1, bf16[512,2048]{1,0:T(8,128)(2,1)} %graph_two_ref.1, f32[512,512]{1,0:T(8,128)} %coupling_ref.1, s32[32]{0:T(128)} %sizes_one_ref.1, s32[4]{0:T(128)} %sizes_two_ref.1), custom_call_target="tpu_custom_call" | custom-call | tf_op jit(solution)/shard_map/gw_step/pallas_call | solution.py:476
  125.5 2.4 %finish.1 = (f32[512,512]{1,0:T(8,128)}, f32[4,128]{1,0:T(4,128)}, f32[4,128]{1,0:T(4,128)}) custom-call(f32[512,512]{1,0:T(8,128)} %get-tuple-element.9.cost_ref, f32[512,128]{1,0:T(8,128)} %get-tuple-element.10.rho_ref, f32[16,128]{1,0:T(8,128)} %get-tuple-element.11.vectors_ref), custom_call_target="tpu_custom_call" | custom-call | tf_op jit(solution)/shard_map/finish/pallas_call | solution.py:511

commit v3 on v2

--- a/solution.py
+++ b/solution.py
@@ -13,11 +13,10 @@
 LANES = 128
 TILES = BLOCK // LANES
 CHUNK = 64
-WIDTHS = (256, 256)
-STEPS = (
-    (0, 0), (-1, 0), (1, 0), (0, -1), (0, 1), (2, 0), (-1, -1), (-1, 1),
-    (1, -1), (1, 1), (0, 2), (2, -1), (2, 1), (-1, 2), (1, 2), (2, 2),
-)
+WIDTH = 256
+PARTS = BLOCK // WIDTH
+OFFSETS = (0, -1, 1, 2)
+STEPS = tuple((first, second) for second in OFFSETS for first in OFFSETS)
 HALF = BLOCK // 2
 UNIT = BLOCK // 4
 MESH = pl.DeviceIdType.MESH
@@ -36,14 +35,78 @@
     return [step[2:] for step in sorted(steps)]
 
 
-def row_index(x, z, core):
-    return (x * 4 + z) * 2 + core
-
-
 def diagonal():
     return lax.broadcasted_iota(jnp.int32, (LANES, LANES), 0) == lax.broadcasted_iota(
         jnp.int32, (LANES, LANES), 1
     )
+
+
+UNIT_US, HOP_US, SLOT_US, AHEAD_US = 1.405, 2.5, 1.0, 2.8
+
+
+def sends_of(part, half, turn, first, second):
+    onward = 1 if turn == 0 else -1
+    out = []
+    if second == 0:
+        if first == 0:
+            for way in (1, -1):
+                out.append((0, way, (-way, 0), 4 if way == onward else 3))
+        elif first == -onward:
+            out.append((0, onward, (2, 0), 3))
+        for way in (1, -1):
+            out.append((1, way, (first, -way), 2 if way == onward else 1))
+    elif second == -onward:
+        out.append((1, onward, (first, 2), 1))
+    return out
+
+
+def timetable():
+    arrival = {
+        (part, half, turn, 0, 0): 0.0
+        for part in range(PARTS)
+        for half in range(2)
+        for turn in range(2)
+    }
+    free = {(axis, way): 0.0 for axis in range(2) for way in (1, -1)}
+    pending, known, slots, now = [], set(), [], 0.0
+    while len(known) < PARTS * 4 * len(STEPS):
+        fresh = sorted(
+            (unit for unit in arrival if arrival[unit] <= now and unit not in known),
+            key=lambda unit: (arrival[unit], unit),
+        )
+        known.update(fresh)
+        for unit in fresh:
+            pending += [(unit, *send) for send in sends_of(*unit)]
+        sends = []
+        for axis, way in free:
+            while max(free[axis, way], now) - now < AHEAD_US:
+                ready = [
+                    send
+                    for send in pending
+                    if send[2] == way and (send[1] + send[0][1]) % 2 == axis
+                ]
+                if not ready:
+                    break
+                best = min(ready, key=lambda send: (send[0][0], -send[4]))
+                pending.remove(best)
+                free[axis, way] = max(free[axis, way], now) + UNIT_US
+                arrival[best[0][:3] + best[3]] = free[axis, way] + HOP_US
+                sends.append(best)
+        slots.append((fresh, sends))
+        now += SLOT_US
+    return slots
+
+
+def items_of(slots):
+    count, work, last = {}, {}, -1
+    for index, (fresh, _) in enumerate(slots):
+        for part, _, _, first, second in fresh:
+            key = (part, STEPS.index((first, second)))
+            count[key] = count.get(key, 0) + 1
+            if count[key] == 4:
+                last = max(index + 2, last + 1)
+                work[last] = key
+    return work
 
 
 def gw_kernel(
@@ -58,11 +121,10 @@
     vectors_ref,
     *scratch,
 ):
-    parts = len(WIDTHS)
-    plans, scratch = scratch[:parts], scratch[parts:]
-    firsts, scratch = scratch[:parts], scratch[parts:]
-    totals, scratch = scratch[:parts], scratch[parts:]
     (
+        plans,
+        firsts,
+        totals,
         one_ref,
         two_ref,
         loaded_ref,
@@ -83,12 +145,21 @@
     row = lax.axis_index("row")
     col = lax.axis_index("col")
     x, z, core = row // 8, (row // 2) % 4, row % 2
+    other = 1 - core
     partner = row + 1 - 2 * core
-    row_peers = [lax.rem(col + step, 4) for step in (2, 1, 3)]
+
+    def around(value):
+        return [value] + [
+            jnp.where(value >= 4 - step, value + step - 4, value + step) for step in (1, 2, 3)
+        ]
+
+    xs, zs = [8 * value for value in around(x)], [2 * value for value in around(z)]
+    _, up, across, down = around(col)
+    row_peers = [across, up, down]
     col_peers = [
-        row_index(lax.rem(x + dx, 4), lax.rem(z + dz, 4), lax.rem(core + dc, 2))
-        for dx, dz, dc in plane_neighbours()
+        xs[dx] + zs[dz] + (other if dc else core) for dx, dz, dc in plane_neighbours()
     ]
+    places = [[xs[dx] + zs[dz] + core for dz in range(4)] for dx in range(4)]
 
     barrier = pltpu.get_barrier_semaphore()
     for peer in row_peers:
@@ -142,107 +213,105 @@
         copy.start()
     for start in range(0, BLOCK, CHUNK):
         rows = pl.ds(start, CHUNK)
-        offset = 0
-        for part, width in enumerate(WIDTHS):
+        for part in range(PARTS):
             kept = jnp.where(
-                live_part(start, width, offset), loaded_ref[rows, pl.ds(offset, width)], 0.0
+                live_part(start, WIDTH, part * WIDTH),
+                loaded_ref[rows, pl.ds(part * WIDTH, WIDTH)],
+                0.0,
             )
-            plans[part][row, rows, :] = kept.astype(jnp.bfloat16)
-            offset += width
+            plans[part, row, rows, :] = kept.astype(jnp.bfloat16)
     squares_ref[...] = jnp.zeros_like(squares_ref)
     pl.semaphore_wait(barrier, 34)
 
     def place(half, first, second):
         dx, dz = (first, second) if half == 0 else (second, first)
-        return row_index(lax.rem(x + dx + 4, 4), lax.rem(z + dz + 4, 4), core)
-
-    def send_unit(part, step, half, turn, source, target):
-        rows = pl.ds(half * HALF + turn * UNIT, UNIT)
-        piece = plans[part].at[source, rows, :]
-        pltpu.make_async_remote_copy(
-            src_ref=piece,
-            dst_ref=piece,
-            send_sem=plan_send.at[part],
-            recv_sem=plan_recv.at[part, step, half, turn],
-            device_id=(target, col),
-            device_id_type=MESH,
-        ).start()
-
-    def send_pair(part, step, half, source):
-        piece = plans[part].at[source, pl.ds(half * HALF, HALF), :]
-        pltpu.make_async_remote_copy(
-            src_ref=piece,
-            dst_ref=piece,
-            send_sem=plan_send.at[part],
-            recv_sem=pair_recv.at[part, step],
-            device_id=(partner, col),
-            device_id_type=MESH,
-        ).start()
+        return places[dx % 4][dz % 4]
 
     def wait_bytes(ref, sem):
         pltpu.make_async_copy(ref, ref, sem).wait()
 
-    def moves(part, step):
-        first, second = STEPS[step]
-        for half in range(2):
-            source = place(half, first, second)
-            for turn in range(2):
-                if (first, second) != (0, 0):
-                    rows = pl.ds(half * HALF + turn * UNIT, UNIT)
-                    wait_bytes(
-                        plans[part].at[source, rows, :], plan_recv.at[part, step, half, turn]
+    def piece_of(part, half, turn, first, second):
+        rows = pl.ds(half * HALF + turn * UNIT, UNIT)
+        return plans.at[part, place(half, first, second), rows, :]
+
+    def moves(fresh, sends):
+        for unit in fresh:
+            part, half, turn, first, second = unit
+            step = STEPS.index((first, second))
+            piece = piece_of(*unit)
+            if (first, second) != (0, 0):
+                wait_bytes(piece, plan_recv.at[part, step, half, turn])
+        for unit, axis, way, seen, _ in sends:
+            part, half, turn, first, second = unit
+            piece = piece_of(*unit)
+            target = place(half, way, 0) if axis == 0 else place(half, 0, way)
+            pltpu.make_async_remote_copy(
+                src_ref=piece,
+                dst_ref=piece,
+                send_sem=plan_send.at[part],
+                recv_sem=plan_recv.at[part, STEPS.index(seen), half, turn],
+                device_id=(target, col),
+                device_id_type=MESH,
+            ).start()
+        for unit in fresh:
+            part, half, turn, first, second = unit
+            piece = piece_of(*unit)
+            pltpu.make_async_remote_copy(
+                src_ref=piece,
+                dst_ref=piece,
+                send_sem=plan_send.at[part],
+                recv_sem=pair_recv.at[part, STEPS.index((first, second))],
+                device_id=(partner, col),
+                device_id_type=MESH,
+            ).start()
+
+    def pick(options, index):
+        value = options[OFFSETS[-1] % 4]
+        for place_of, offset in enumerate(OFFSETS[:-1]):
+            value = jnp.where(index == place_of, options[offset % 4], value)
+        return value
+
+    def multiply(code):
+        part = jnp.where(code >= len(STEPS), 1, 0)
+        step = code - len(STEPS) * part
+        second = (
+            jnp.where(step >= 4, 1, 0) + jnp.where(step >= 8, 1, 0) + jnp.where(step >= 12, 1, 0)
+        )
+        first = step - 4 * second
+        wait_bytes(plans.at[0, 0], pair_recv.at[part, step])
+        chips = (pick(xs, first) + pick(zs, second), pick(xs, second) + pick(zs, first))
+        for start in range(0, BLOCK, HALF):
+            total = totals[part, pl.ds(start, HALF), :]
+            for half in range(2):
+                rows = pl.ds(half * HALF, HALF)
+                for owner in (core, other):
+                    source = chips[half] + owner
+                    total = total + jnp.dot(
+                        one_ref[source, pl.ds(start, HALF), rows],
+                        plans[part, source, rows, :],
+                        preferred_element_type=jnp.float32,
                     )
-                onward = -1 if turn == 0 else 1
-                if second == 0:
-                    for sent in (-1, 1):
-                        if first == 0 or (first == onward and sent == onward):
-                            seen = sent if first == 0 else 2
-                            send_unit(
-                                part, STEPS.index((seen, 0)), half, turn, source,
-                                place(half, -sent, 0),
-                            )
-                    for sent in (-1, 1):
-                        send_unit(
-                            part, STEPS.index((first, sent)), half, turn, source,
-                            place(half, 0, -sent),
-                        )
-                elif second == onward:
-                    send_unit(
-                        part, STEPS.index((first, 2)), half, turn, source, place(half, 0, -onward)
-                    )
-            send_pair(part, step, half, source)
-
-    def offset_of(step, axis):
-        value = jnp.int32(STEPS[-1][axis])
-        for index in range(len(STEPS) - 1):
-            value = jnp.where(step == index, jnp.int32(STEPS[index][axis]), value)
-        return value
-
-    def multiply(part, step, parity):
-        first, second = offset_of(step, 0), offset_of(step, 1)
-        for half in range(2):
-            source = place(half, first, second)
-            source = source + parity * (1 - 2 * core)
-            rows = pl.ds(half * HALF, HALF)
-            left = one_ref[source, :, rows]
-            totals[part][...] += jnp.dot(
-                left, plans[part][source, rows, :], preferred_element_type=jnp.float32
-            )
-            if part == 0:
-                size = sizes_one_ref[source]
-                for start in range(0, BLOCK, CHUNK):
-                    squares = squares_ref[pl.ds(start, CHUNK), :]
-                    for tile in range(2):
-                        lanes = half * HALF + tile * LANES
-                        ids = lax.broadcasted_iota(jnp.int32, (CHUNK, LANES), 1) + lanes
-                        value = one_ref[source, pl.ds(start, CHUNK), pl.ds(lanes, LANES)].astype(
-                            jnp.float32
-                        )
-                        squares = squares + jnp.where(ids < size, value * value, 0.0)
-                    squares_ref[pl.ds(start, CHUNK), :] = squares
+            totals[part, pl.ds(start, HALF), :] = total
+
+        @pl.when(part == 0)
+        def _():
+            for start in range(0, BLOCK, CHUNK):
+                squares = squares_ref[pl.ds(start, CHUNK), :]
+                for half in range(2):
+                    for owner in (core, other):
+                        source = chips[half] + owner
+                        size = sizes_one_ref[source]
+                        for tile in range(2):
+                            lanes = half * HALF + tile * LANES
+                            ids = lax.broadcasted_iota(jnp.int32, (CHUNK, LANES), 1) + lanes
+                            value = one_ref[
+                                source, pl.ds(start, CHUNK), pl.ds(lanes, LANES)
+                            ].astype(jnp.float32)
+                            squares = squares + jnp.where(ids < size, value * value, 0.0)
+                squares_ref[pl.ds(start, CHUNK), :] = squares
 
     def first_copy(part, half, source, key, target):
-        piece = firsts[part].at[source, pl.ds(half * HALF, HALF), :]
+        piece = firsts.at[part, source, pl.ds(half * HALF, HALF), :]
         return pltpu.make_async_remote_copy(
             src_ref=piece,
             dst_ref=piece,
@@ -252,19 +321,17 @@
             device_id_type=MESH,
         )
 
-    up, down, across = lax.rem(col + 1, 4), lax.rem(col + 3, 4), lax.rem(col + 2, 4)
-
     def first_start(part):
         for start in range(0, BLOCK, CHUNK):
             rows = pl.ds(start, CHUNK)
-            firsts[part][col, rows, :] = totals[part][rows, :].astype(jnp.bfloat16)
+            firsts[part, col, rows, :] = totals[part, rows, :].astype(jnp.bfloat16)
         first_copy(part, 0, col, 0, up).start()
         first_copy(part, 1, col, 1, down).start()
         first_copy(part, 1, col, 2, up).start()
         first_copy(part, 0, col, 3, down).start()
 
     def first_wait(part, half, source, key):
-        wait_bytes(firsts[part].at[source, pl.ds(half * HALF, HALF), :], first_recv.at[part, key])
+        wait_bytes(firsts.at[part, source, pl.ds(half * HALF, HALF), :], first_recv.at[part, key])
 
     def first_onward(part):
         first_wait(part, 0, down, 0)
@@ -273,10 +340,9 @@
         first_copy(part, 1, up, 5, down).start()
 
     def cross_add(part, source, fresh=False):
-        offset = sum(WIDTHS[:part])
         added = lax.dot_general(
-            firsts[part][source],
-            two_ref[source, :, pl.ds(offset, WIDTHS[part])],
+            firsts[part, source],
+            two_ref[source, :, pl.ds(part * WIDTH, WIDTH)],
             (((1,), (1,)), ((), ())),
             preferred_element_type=jnp.float32,
         )
@@ -295,12 +361,18 @@
         first_wait(part, 1, across, 5)
         cross_add(part, across)
 
-    last = len(STEPS) - 1
-    for part in range(parts):
-        totals[part][...] = jnp.zeros_like(totals[part])
-    moves(0, 0)
-    if parts > 1:
-        moves(1, 0)
+    slots = timetable()
+    work = items_of(slots)
+    length = max(work) + 1
+    slots = slots + [([], [])] * (length - len(slots))
+    whole = [max(slot for slot in work if work[slot][0] == part) for part in range(PARTS)]
+    extra = {}
+    for part in range(PARTS - 1):
+        extra[whole[part] + 1] = [functools.partial(first_start, part)]
+        extra[whole[part] + 8] = [functools.partial(first_onward, part)]
+        extra[whole[part] + 16] = [functools.partial(first_end, part)]
+    totals[...] = jnp.zeros_like(totals)
+    moves(*slots[0])
     wait_bytes(two_ref, load_sem.at[1])
     col_square = []
     for tile in range(TILES):
@@ -324,35 +396,33 @@
         )
     wait_bytes(one_ref, load_sem.at[2])
 
-    for part in range(parts):
-
-        def one_step(step, carry, part=part):
-            for index in range(1, len(STEPS)):
-
-                @pl.when(step == index)
-                def _():
-                    moves(part, index)
-                    if index == 6 and 1 < part + 1 < parts:
-                        moves(part + 1, 0)
-                    if part and index == 5:
-                        first_onward(part - 1)
-                    if part and index == 11:
-                        first_end(part - 1)
-
-            multiply(part, step, 0)
-
-            @pl.when(step > 0)
+    def one_slot(slot, carry):
+        for group in range(0, length, 8):
+
+            @pl.when((slot >= group) & (slot < group + 8))
             def _():
-                wait_bytes(plans[part].at[0], pair_recv.at[part, lax.max(step - 1, 0)])
-                multiply(part, lax.max(step - 1, 0), 1)
-
-            return carry
-
-        lax.fori_loop(0, len(STEPS), one_step, 0)
-        wait_bytes(plans[part].at[0], pair_recv.at[part, last])
-        multiply(part, last, 1)
-        first_start(part)
-    first_onward(parts - 1)
+                for index in range(max(group, 1), min(group + 8, length)):
+                    if slots[index] != ([], []) or index in extra:
+
+                        @pl.when(slot == index)
+                        def _():
+                            moves(*slots[index])
+                            for run in extra.get(index, ()):
+                                run()
+
+        code = jnp.int32(-1)
+        for index, (part, step) in work.items():
+            code = jnp.where(slot == index, part * len(STEPS) + step, code)
+
+        @pl.when(code >= 0)
+        def _():
+            multiply(code)
+
+        return carry
+
+    lax.fori_loop(0, length, one_slot, 0)
+    first_start(PARTS - 1)
+    first_onward(PARTS - 1)
     for tile in range(TILES):
         column = jnp.broadcast_to(
             jnp.sum(squares_ref[pl.ds(tile * LANES, LANES), :], axis=1, keepdims=True),
@@ -361,7 +431,7 @@
         vectors_ref[pl.ds(8 + tile, 1), :] = jnp.sum(
             jnp.where(diag, column, 0.0), axis=0, keepdims=True
         )
-    first_end(parts - 1)
+    first_end(PARTS - 1)
 
     scale = jnp.float32(2.0 / math.sqrt(mass_scale) * math.log2(math.e))
     for start in range(0, BLOCK, CHUNK):
@@ -448,9 +518,9 @@
         return carry
 
     lax.fori_loop(0, SWEEPS, drain, 0)
-    for part in range(parts):
-        wait_bytes(plans[part].at[pl.ds(0, 31)], plan_send.at[part])
-        wait_bytes(firsts[part].at[pl.ds(0, 3)], first_send.at[part])
+    for part in range(PARTS):
+        wait_bytes(plans.at[part, pl.ds(0, 31)], plan_send.at[part])
+        wait_bytes(firsts.at[part, pl.ds(0, 3)], first_send.at[part])
 
 
 def finish_kernel(mass_scale, cost_ref, rho_ref, vectors_ref, plan_ref, row_ref, col_ref):
@@ -470,7 +540,6 @@
     vmem = pl.BlockSpec(memory_space=pltpu.VMEM)
     smem = pl.BlockSpec(memory_space=pltpu.SMEM)
     hbm = pl.BlockSpec(memory_space=pltpu.HBM)
-    parts = len(WIDTHS)
     f32, bf16 = jnp.float32, jnp.bfloat16
     dma = pltpu.SemaphoreType.DMA
     cost, rho, vectors = pl.pallas_call(
@@ -483,9 +552,9 @@
         in_specs=[hbm, hbm, hbm, smem, smem],
         out_specs=(vmem, vmem, vmem),
         scratch_shapes=[
-            *(pltpu.VMEM((32, BLOCK, width), bf16) for width in WIDTHS),
-            *(pltpu.VMEM((4, BLOCK, width), bf16) for width in WIDTHS),
-            *(pltpu.VMEM((BLOCK, width), f32) for width in WIDTHS),
+            pltpu.VMEM((PARTS, 32, BLOCK, WIDTH), bf16),
+            pltpu.VMEM((PARTS, 4, BLOCK, WIDTH), bf16),
+            pltpu.VMEM((PARTS, BLOCK, WIDTH), f32),
             pltpu.VMEM((32, BLOCK, BLOCK), bf16),
             pltpu.VMEM((4, BLOCK, BLOCK), bf16),
             pltpu.VMEM((BLOCK, BLOCK), f32),
@@ -493,11 +562,11 @@
             pltpu.VMEM((SWEEPS, 4, TILES, LANES), f32),
             pltpu.VMEM((SWEEPS, 32, TILES, LANES), f32),
             dma((3,)),
-            dma((parts,)),
-            dma((parts, len(STEPS), 2, 2)),
-            dma((parts, len(STEPS))),
-            dma((parts,)),
-            dma((parts, 6)),
+            dma((PARTS,)),
+            dma((PARTS, len(STEPS), 2, 2)),
+            dma((PARTS, len(STEPS))),
+            dma((PARTS,)),
+            dma((PARTS, 6)),
             dma((SWEEPS,)),
             dma((SWEEPS,)),
             dma((SWEEPS,)),

time: 128 us -> 120 us (0.938)
  Pallas kernels: 127 us -> 119 us
    pallas_call x1, Pallas kernels: 125 us -> 116 us  [body(): pl.pallas_call(functools.partial(gw_kernel, mass_scale), out_shape=(jax.S...]
where the time goes in v3:
time: 120 us; the launch traced here: 119 us
  Pallas kernels  119 us (99%)
    pallas_call x1, Pallas kernels, body(): pl.pallas_call(functools.partial(gw_kernel, mass_scale), out_shape=(jax.S...  116 us
    pallas_call x1, Pallas kernels, body(): pl.pallas_call(functools.partial(finish_kernel, mass_scale), out_shape=(j...  2.43 us

profile of v3, /device:TPU:1, one launch (start us, length us, event | category | flops | bytes accessed | tf_op | source)
XLA Modules:
  0.0 119.4 jit_solution(8073288165546377133)
XLA Ops:
  0.6 116.3 %gw_step.1 = (f32[512,512]{1,0:T(8,128)}, f32[512,128]{1,0:T(8,128)}, f32[16,128]{1,0:T(8,128)}) custom-call(bf16[512,16384]{1,0:T(8,128)(2,1)} %graph_one_ref.1, bf16[512,2048]{1,0:T(8,128)(2,1)} %graph_two_ref.1, f32[512,512]{1,0:T(8,128)} %coupling_ref.1, s32[32]{0:T(128)} %sizes_one_ref.1, s32[4]{0:T(128)} %sizes_two_ref.1), custom_call_target="tpu_custom_call" | custom-call | tf_op jit(solution)/shard_map/gw_step/pallas_call | solution.py:545
  117.0 2.4 %finish.1 = (f32[512,512]{1,0:T(8,128)}, f32[4,128]{1,0:T(4,128)}, f32[4,128]{1,0:T(4,128)}) custom-call(f32[512,512]{1,0:T(8,128)} %get-tuple-element.9.cost_ref, f32[512,128]{1,0:T(8,128)} %get-tuple-element.10.rho_ref, f32[16,128]{1,0:T(8,128)} %get-tuple-element.11.vectors_ref), custom_call_target="tpu_custom_call" | custom-call | tf_op jit(solution)/shard_map/finish/pallas_call | solution.py:580

commit v4 on v3

--- a/solution.py
+++ b/solution.py
@@ -13,12 +13,15 @@
 LANES = 128
 TILES = BLOCK // LANES
 CHUNK = 64
-WIDTH = 256
-PARTS = BLOCK // WIDTH
+WIDTHS = (384, 128)
+BEGINS = (0, 384)
+PARTS = len(WIDTHS)
 OFFSETS = (0, -1, 1, 2)
 STEPS = tuple((first, second) for second in OFFSETS for first in OFFSETS)
 HALF = BLOCK // 2
 UNIT = BLOCK // 4
+AFTER = ((1, 8, 40),)
+LAG = 2
 MESH = pl.DeviceIdType.MESH
 
 very_low = -1e30
@@ -41,7 +44,7 @@
     )
 
 
-UNIT_US, HOP_US, SLOT_US, AHEAD_US = 1.405, 2.5, 1.0, 2.8
+COLUMN_US, HOP_US, SLOT_US, AHEAD_US = 1.405 / 256, 2.5, 1.0, 2.8
 
 
 def sends_of(part, half, turn, first, second):
@@ -89,7 +92,9 @@
                     break
                 best = min(ready, key=lambda send: (send[0][0], -send[4]))
                 pending.remove(best)
-                free[axis, way] = max(free[axis, way], now) + UNIT_US
+                free[axis, way] = (
+                    max(free[axis, way], now) + COLUMN_US * WIDTHS[best[0][0]]
+                )
                 arrival[best[0][:3] + best[3]] = free[axis, way] + HOP_US
                 sends.append(best)
         slots.append((fresh, sends))
@@ -97,16 +102,46 @@
     return slots
 
 
+def group_of(unit):
+    part, half, turn, first, second = unit
+    if second == 2:
+        return (part, first, second)
+    if second and second != (-1 if turn == 0 else 1):
+        return (part, turn, first, second)
+    return unit
+
+
+def grouped(slots):
+    size, seen, out = {}, {}, []
+    for fresh, _ in slots:
+        for unit in fresh:
+            size[group_of(unit)] = size.get(group_of(unit), 0) + 1
+    for fresh, sends in slots:
+        ready = []
+        for unit in fresh:
+            group = group_of(unit)
+            seen.setdefault(group, []).append(unit)
+            if len(seen[group]) == size[group]:
+                ready.append((group, seen[group]))
+        out.append((ready, sends))
+    return out, {group: index for index, group in enumerate(size) if group[-2:] != (0, 0)}
+
+
 def items_of(slots):
     count, work, last = {}, {}, -1
-    for index, (fresh, _) in enumerate(slots):
-        for part, _, _, first, second in fresh:
+    for index, (ready, _) in enumerate(slots):
+        for part, _, _, first, second in (unit for _, units in ready for unit in units):
             key = (part, STEPS.index((first, second)))
             count[key] = count.get(key, 0) + 1
             if count[key] == 4:
-                last = max(index + 2, last + 1)
+                pace = 2 if part == 0 else 1
+                last = max(2 * (index + LAG), last + pace)
                 work[last] = key
     return work
+
+
+def plan_of_moves():
+    return grouped(timetable())
 
 
 def gw_kernel(
@@ -122,9 +157,12 @@
     *scratch,
 ):
     (
-        plans,
-        firsts,
-        totals,
+        plan_wide,
+        plan_slim,
+        first_wide,
+        first_slim,
+        total_wide,
+        total_slim,
         one_ref,
         two_ref,
         loaded_ref,
@@ -132,6 +170,7 @@
         row_box,
         col_box,
         load_sem,
+        one_sem,
         plan_send,
         plan_recv,
         pair_recv,
@@ -142,6 +181,11 @@
         col_send,
         col_recv,
     ) = scratch
+    plans = [plan_wide, plan_slim]
+    firsts = [first_wide, first_slim]
+    totals = [total_wide, total_slim]
+    load_coupling = pltpu.make_async_copy(coupling_ref, loaded_ref, load_sem.at[0])
+    load_coupling.start()
     row = lax.axis_index("row")
     col = lax.axis_index("col")
     x, z, core = row // 8, (row // 2) % 4, row % 2
@@ -167,8 +211,6 @@
     for peer in col_peers:
         pl.semaphore_signal(barrier, inc=1, device_id=(peer, col), device_id_type=MESH)
 
-    load_coupling = pltpu.make_async_copy(coupling_ref, loaded_ref, load_sem.at[0])
-    load_coupling.start()
     load_two = []
     for block in range(4):
         load_two.append(
@@ -176,14 +218,6 @@
                 graph_two_ref.at[:, pl.ds(block * BLOCK, BLOCK)], two_ref.at[block], load_sem.at[1]
             )
         )
-    load_one = []
-    for block in range(32):
-        load_one.append(
-            pltpu.make_async_copy(
-                graph_one_ref.at[:, pl.ds(block * BLOCK, BLOCK)], one_ref.at[block], load_sem.at[2]
-            )
-        )
-
     total_one = jnp.float32(0)
     for block in range(sizes_one_ref.shape[0]):
         total_one = total_one + sizes_one_ref[block].astype(jnp.float32)
@@ -209,17 +243,15 @@
         return (ids < size_one) & (lanes < size_two)
 
     load_coupling.wait()
-    for copy in load_two + load_one:
-        copy.start()
     for start in range(0, BLOCK, CHUNK):
         rows = pl.ds(start, CHUNK)
         for part in range(PARTS):
             kept = jnp.where(
-                live_part(start, WIDTH, part * WIDTH),
-                loaded_ref[rows, pl.ds(part * WIDTH, WIDTH)],
+                live_part(start, WIDTHS[part], BEGINS[part]),
+                loaded_ref[rows, pl.ds(BEGINS[part], WIDTHS[part])],
                 0.0,
             )
-            plans[part, row, rows, :] = kept.astype(jnp.bfloat16)
+            plans[part][row, rows, :] = kept.astype(jnp.bfloat16)
     squares_ref[...] = jnp.zeros_like(squares_ref)
     pl.semaphore_wait(barrier, 34)
 
@@ -232,15 +264,13 @@
 
     def piece_of(part, half, turn, first, second):
         rows = pl.ds(half * HALF + turn * UNIT, UNIT)
-        return plans.at[part, place(half, first, second), rows, :]
-
-    def moves(fresh, sends):
-        for unit in fresh:
-            part, half, turn, first, second = unit
-            step = STEPS.index((first, second))
-            piece = piece_of(*unit)
-            if (first, second) != (0, 0):
-                wait_bytes(piece, plan_recv.at[part, step, half, turn])
+        return plans[part].at[place(half, first, second), rows, :]
+
+    def moves(ready, sends, fetched):
+        for group, units in ready:
+            if group in semaphores:
+                rows = pl.ds(0, UNIT * len(units))
+                wait_bytes(plans[group[0]].at[0, rows, :], plan_recv.at[semaphores[group]])
         for unit, axis, way, seen, _ in sends:
             part, half, turn, first, second = unit
             piece = piece_of(*unit)
@@ -249,11 +279,11 @@
                 src_ref=piece,
                 dst_ref=piece,
                 send_sem=plan_send.at[part],
-                recv_sem=plan_recv.at[part, STEPS.index(seen), half, turn],
+                recv_sem=plan_recv.at[semaphores[group_of((part, half, turn, *seen))]],
                 device_id=(target, col),
                 device_id_type=MESH,
             ).start()
-        for unit in fresh:
+        for unit in (unit for _, units in ready for unit in units):
             part, half, turn, first, second = unit
             piece = piece_of(*unit)
             pltpu.make_async_remote_copy(
@@ -264,6 +294,16 @@
                 device_id=(partner, col),
                 device_id_type=MESH,
             ).start()
+        for step in fetched:
+            for half in range(2):
+                for owner in (core, other):
+                    source = place(half, *STEPS[step]) - core + owner
+                    start = pl.multiple_of(source * BLOCK + half * HALF, HALF)
+                    pltpu.make_async_copy(
+                        graph_one_ref.at[:, pl.ds(start, HALF)],
+                        one_ref.at[source, :, pl.ds(half * HALF, HALF)],
+                        one_sem.at[step],
+                    ).start()
 
     def pick(options, index):
         value = options[OFFSETS[-1] % 4]
@@ -278,23 +318,32 @@
             jnp.where(step >= 4, 1, 0) + jnp.where(step >= 8, 1, 0) + jnp.where(step >= 12, 1, 0)
         )
         first = step - 4 * second
-        wait_bytes(plans.at[0, 0], pair_recv.at[part, step])
         chips = (pick(xs, first) + pick(zs, second), pick(xs, second) + pick(zs, first))
-        for start in range(0, BLOCK, HALF):
-            total = totals[part, pl.ds(start, HALF), :]
-            for half in range(2):
-                rows = pl.ds(half * HALF, HALF)
-                for owner in (core, other):
-                    source = chips[half] + owner
-                    total = total + jnp.dot(
-                        one_ref[source, pl.ds(start, HALF), rows],
-                        plans[part, source, rows, :],
-                        preferred_element_type=jnp.float32,
-                    )
-            totals[part, pl.ds(start, HALF), :] = total
+
+        def add_products(plan, total_ref):
+            for start in range(0, BLOCK, HALF):
+                total = total_ref[pl.ds(start, HALF), :]
+                for half in range(2):
+                    rows = pl.ds(half * HALF, HALF)
+                    for owner in (core, other):
+                        source = chips[half] + owner
+                        total = total + jnp.dot(
+                            one_ref[source, pl.ds(start, HALF), rows],
+                            plan[source, rows, :],
+                            preferred_element_type=jnp.float32,
+                        )
+                total_ref[pl.ds(start, HALF), :] = total
+
+        @pl.when(part > 0)
+        def _():
+            wait_bytes(plan_slim.at[0], pair_recv.at[part, step])
+            add_products(plan_slim, total_slim)
 
         @pl.when(part == 0)
         def _():
+            wait_bytes(plan_wide.at[0], pair_recv.at[part, step])
+            wait_bytes(one_ref.at[pl.ds(0, 2)], one_sem.at[step])
+            add_products(plan_wide, total_wide)
             for start in range(0, BLOCK, CHUNK):
                 squares = squares_ref[pl.ds(start, CHUNK), :]
                 for half in range(2):
@@ -311,7 +360,7 @@
                 squares_ref[pl.ds(start, CHUNK), :] = squares
 
     def first_copy(part, half, source, key, target):
-        piece = firsts.at[part, source, pl.ds(half * HALF, HALF), :]
+        piece = firsts[part].at[source, pl.ds(half * HALF, HALF), :]
         return pltpu.make_async_remote_copy(
             src_ref=piece,
             dst_ref=piece,
@@ -324,14 +373,14 @@
     def first_start(part):
         for start in range(0, BLOCK, CHUNK):
             rows = pl.ds(start, CHUNK)
-            firsts[part, col, rows, :] = totals[part, rows, :].astype(jnp.bfloat16)
+            firsts[part][col, rows, :] = totals[part][rows, :].astype(jnp.bfloat16)
         first_copy(part, 0, col, 0, up).start()
         first_copy(part, 1, col, 1, down).start()
         first_copy(part, 1, col, 2, up).start()
         first_copy(part, 0, col, 3, down).start()
 
     def first_wait(part, half, source, key):
-        wait_bytes(firsts.at[part, source, pl.ds(half * HALF, HALF), :], first_recv.at[part, key])
+        wait_bytes(firsts[part].at[source, pl.ds(half * HALF, HALF), :], first_recv.at[part, key])
 
     def first_onward(part):
         first_wait(part, 0, down, 0)
@@ -341,8 +390,8 @@
 
     def cross_add(part, source, fresh=False):
         added = lax.dot_general(
-            firsts[part, source],
-            two_ref[source, :, pl.ds(part * WIDTH, WIDTH)],
+            firsts[part][source],
+            two_ref[source, :, pl.ds(BEGINS[part], WIDTHS[part])],
             (((1,), (1,)), ((), ())),
             preferred_element_type=jnp.float32,
         )
@@ -361,18 +410,24 @@
         first_wait(part, 1, across, 5)
         cross_add(part, across)
 
-    slots = timetable()
+    slots, semaphores = plan_of_moves()
     work = items_of(slots)
-    length = max(work) + 1
+    length = max(work) // 2 + 1
     slots = slots + [([], [])] * (length - len(slots))
-    whole = [max(slot for slot in work if work[slot][0] == part) for part in range(PARTS)]
+    order = [work[turn][1] for turn in sorted(work) if work[turn][0] == 0]
+    fetches = [order[:4]] + [[step] for step in order[4:]] + [[]] * length
+    whole = [max(turn // 2 for turn in work if work[turn][0] == part) for part in range(PARTS)]
     extra = {}
     for part in range(PARTS - 1):
-        extra[whole[part] + 1] = [functools.partial(first_start, part)]
-        extra[whole[part] + 8] = [functools.partial(first_onward, part)]
-        extra[whole[part] + 16] = [functools.partial(first_end, part)]
-    totals[...] = jnp.zeros_like(totals)
-    moves(*slots[0])
+        for after, run in zip(AFTER[part], (first_start, first_onward, first_end)):
+            extra.setdefault(min(whole[part] + after, length), []).append(
+                functools.partial(run, part)
+            )
+    for total in totals:
+        total[...] = jnp.zeros_like(total)
+    moves(*slots[0], fetches[0])
+    for copy in load_two:
+        copy.start()
     wait_bytes(two_ref, load_sem.at[1])
     col_square = []
     for tile in range(TILES):
@@ -394,7 +449,6 @@
         vectors_ref[pl.ds(12 + tile, 1), :] = jnp.sum(
             jnp.where(diag, jnp.concatenate(summed, axis=0), 0.0), axis=0, keepdims=True
         )
-    wait_bytes(one_ref, load_sem.at[2])
 
     def one_slot(slot, carry):
         for group in range(0, length, 8):
@@ -402,27 +456,31 @@
             @pl.when((slot >= group) & (slot < group + 8))
             def _():
                 for index in range(max(group, 1), min(group + 8, length)):
-                    if slots[index] != ([], []) or index in extra:
+                    if slots[index] != ([], []) or fetches[index] or index in extra:
 
                         @pl.when(slot == index)
                         def _():
-                            moves(*slots[index])
+                            moves(*slots[index], fetches[index])
                             for run in extra.get(index, ()):
                                 run()
 
-        code = jnp.int32(-1)
-        for index, (part, step) in work.items():
-            code = jnp.where(slot == index, part * len(STEPS) + step, code)
-
-        @pl.when(code >= 0)
-        def _():
-            multiply(code)
-
-        return carry
+        def one_turn(turn, carry):
+            code = jnp.int32(-1)
+            for index, (part, step) in work.items():
+                code = jnp.where(2 * slot + turn == index, part * len(STEPS) + step, code)
+
+            @pl.when(code >= 0)
+            def _():
+                multiply(code)
+
+            return carry
+
+        return lax.fori_loop(0, 2, one_turn, carry)
 
     lax.fori_loop(0, length, one_slot, 0)
     first_start(PARTS - 1)
-    first_onward(PARTS - 1)
+    for run in extra.get(length, ()):
+        run()
     for tile in range(TILES):
         column = jnp.broadcast_to(
             jnp.sum(squares_ref[pl.ds(tile * LANES, LANES), :], axis=1, keepdims=True),
@@ -431,6 +489,7 @@
         vectors_ref[pl.ds(8 + tile, 1), :] = jnp.sum(
             jnp.where(diag, column, 0.0), axis=0, keepdims=True
         )
+    first_onward(PARTS - 1)
     first_end(PARTS - 1)
 
     scale = jnp.float32(2.0 / math.sqrt(mass_scale) * math.log2(math.e))
@@ -445,7 +504,7 @@
             pltpu.make_async_remote_copy(
                 src_ref=box.at[sweep, mine],
                 dst_ref=box.at[sweep, mine],
-                send_sem=send.at[sweep],
+                send_sem=send.at[0],
                 recv_sem=recv.at[sweep],
                 device_id=target,
                 device_id_type=MESH,
@@ -512,15 +571,11 @@
     vectors_ref[pl.ds(8, TILES), :] = jnp.where(live_row, rho * unit + row_const, 0.0)
     vectors_ref[pl.ds(12, TILES), :] = jnp.where(live_col, gamma * unit + col_const, 0.0)
 
-    def drain(sweep, carry):
-        for box, send, count in ((row_box, row_send, 3), (col_box, col_send, 31)):
-            wait_bytes(box.at[sweep, pl.ds(0, count)], send.at[sweep])
-        return carry
-
-    lax.fori_loop(0, SWEEPS, drain, 0)
+    wait_bytes(row_box.at[:, pl.ds(0, 3)], row_send.at[0])
+    wait_bytes(col_box.at[:, pl.ds(0, 31)], col_send.at[0])
     for part in range(PARTS):
-        wait_bytes(plans.at[part, pl.ds(0, 31)], plan_send.at[part])
-        wait_bytes(firsts.at[part, pl.ds(0, 3)], first_send.at[part])
+        wait_bytes(plans[part].at[pl.ds(0, 31)], plan_send.at[part])
+        wait_bytes(firsts[part].at[pl.ds(0, 3)], first_send.at[part])
 
 
 def finish_kernel(mass_scale, cost_ref, rho_ref, vectors_ref, plan_ref, row_ref, col_ref):
@@ -536,6 +591,10 @@
 
 
 def body(graph_one, graph_two, coupling, sizes_one, sizes_two):
+    graph_one, graph_two, coupling, sizes_one, sizes_two = (
+        pltpu.with_memory_space_constraint(value, pltpu.HBM)
+        for value in (graph_one, graph_two, coupling, sizes_one, sizes_two)
+    )
     mass_scale = float(graph_one.shape[1] * graph_two.shape[1])
     vmem = pl.BlockSpec(memory_space=pltpu.VMEM)
     smem = pl.BlockSpec(memory_space=pltpu.SMEM)
@@ -552,28 +611,32 @@
         in_specs=[hbm, hbm, hbm, smem, smem],
         out_specs=(vmem, vmem, vmem),
         scratch_shapes=[
-            pltpu.VMEM((PARTS, 32, BLOCK, WIDTH), bf16),
-            pltpu.VMEM((PARTS, 4, BLOCK, WIDTH), bf16),
-            pltpu.VMEM((PARTS, BLOCK, WIDTH), f32),
+            pltpu.VMEM((32, BLOCK, WIDTHS[0]), bf16),
+            pltpu.VMEM((32, BLOCK, WIDTHS[1]), bf16),
+            pltpu.VMEM((4, BLOCK, WIDTHS[0]), bf16),
+            pltpu.VMEM((4, BLOCK, WIDTHS[1]), bf16),
+            pltpu.VMEM((BLOCK, WIDTHS[0]), f32),
+            pltpu.VMEM((BLOCK, WIDTHS[1]), f32),
             pltpu.VMEM((32, BLOCK, BLOCK), bf16),
             pltpu.VMEM((4, BLOCK, BLOCK), bf16),
             pltpu.VMEM((BLOCK, BLOCK), f32),
             pltpu.VMEM((BLOCK, LANES), f32),
             pltpu.VMEM((SWEEPS, 4, TILES, LANES), f32),
             pltpu.VMEM((SWEEPS, 32, TILES, LANES), f32),
-            dma((3,)),
+            dma((2,)),
+            dma((len(STEPS),)),
             dma((PARTS,)),
-            dma((PARTS, len(STEPS), 2, 2)),
+            dma((len(plan_of_moves()[1]) + 4 * PARTS,)),
             dma((PARTS, len(STEPS))),
             dma((PARTS,)),
             dma((PARTS, 6)),
+            dma((1,)),
             dma((SWEEPS,)),
-            dma((SWEEPS,)),
-            dma((SWEEPS,)),
+            dma((1,)),
             dma((SWEEPS,)),
         ],
         compiler_params=pltpu.CompilerParams(
-            collective_id=0, has_side_effects=True, vmem_limit_bytes=56 * 1024 * 1024
+            collective_id=0, has_side_effects=True, vmem_limit_bytes=52000 * 1024
         ),
         name="gw_step",
     )(graph_one, graph_two, coupling, sizes_one, sizes_two)
@@ -586,6 +649,7 @@
         ),
         in_specs=[vmem, vmem, vmem],
         out_specs=(vmem, vmem, vmem),
+        compiler_params=pltpu.CompilerParams(vmem_limit_bytes=8 * 1024 * 1024),
         name="finish",
     )(cost, rho, vectors)
     return plan, row_potential.reshape(BLOCK), col_potential.reshape(BLOCK)

time: 120 us -> 115 us (0.958)
  Pallas kernels: 119 us -> 114 us
    pallas_call x1, Pallas kernels: 116 us -> 113 us  [body(): pl.pallas_call(functools.partial(gw_kernel, mass_scale), out_shape=(jax.S...]
    pallas_call x1, Pallas kernels: 2.43 us -> 1.12 us  [body(): pl.pallas_call(functools.partial(finish_kernel, mass_scale), out_shape=(j...]
where the time goes in v4:
time: 115 us
  Pallas kernels  114 us (99%)
    pallas_call x1, Pallas kernels, body(): pl.pallas_call(functools.partial(gw_kernel, mass_scale), out_shape=(jax.S...  113 us

profile of v4, /device:TPU:1, one launch (start us, length us, event | category | flops | bytes accessed | tf_op | source)
XLA Modules:
  0.0 114.9 jit_solution(3741436530190707444)
XLA Ops:
  0.6 113.2 %gw_step.1 = (f32[512,512]{1,0:T(8,128)S(1)}, f32[512,128]{1,0:T(8,128)S(1)}, f32[16,128]{1,0:T(8,128)S(1)}) custom-call(bf16[512,16384]{1,0:T(8,128)(2,1)} %graph_one_ref.1, bf16[512,2048]{1,0:T(8,128)(2,1)} %graph_two_ref.1, f32[512,512]{1,0:T(8,128)} %coupling_ref.1, s32[32]{0:T(128)} %sizes_one_ref.1, s32[4]{0:T(128)} %sizes_two_ref.1), custom_call_target="tpu_custom_call" | custom-call | tf_op jit(solution)/shard_map/gw_step/pallas_call | solution.py:604
  113.8 1.1 finish.1

commit v5 on v4

--- a/solution.py
+++ b/solution.py
@@ -124,7 +124,8 @@
             if len(seen[group]) == size[group]:
                 ready.append((group, seen[group]))
         out.append((ready, sends))
-    return out, {group: index for index, group in enumerate(size) if group[-2:] != (0, 0)}
+    groups = [group for group in size if group[-2:] != (0, 0)]
+    return out, {group: index for index, group in enumerate(groups)}
 
 
 def items_of(slots):
@@ -206,9 +207,9 @@
     places = [[xs[dx] + zs[dz] + core for dz in range(4)] for dx in range(4)]
 
     barrier = pltpu.get_barrier_semaphore()
-    for peer in row_peers:
+    for peer in (up, down):
         pl.semaphore_signal(barrier, inc=1, device_id=(row, peer), device_id_type=MESH)
-    for peer in col_peers:
+    for peer in (places[1][0], places[3][0], places[0][1], places[0][3], partner):
         pl.semaphore_signal(barrier, inc=1, device_id=(peer, col), device_id_type=MESH)
 
     load_two = []
@@ -253,7 +254,7 @@
             )
             plans[part][row, rows, :] = kept.astype(jnp.bfloat16)
     squares_ref[...] = jnp.zeros_like(squares_ref)
-    pl.semaphore_wait(barrier, 34)
+    pl.semaphore_wait(barrier, 7)
 
     def place(half, first, second):
         dx, dz = (first, second) if half == 0 else (second, first)
@@ -410,6 +411,29 @@
         first_wait(part, 1, across, 5)
         cross_add(part, across)
 
+    def square_columns():
+        wait_bytes(two_ref, load_sem.at[1])
+        col_square = []
+        for tile in range(TILES):
+            summed = []
+            for start in range(tile * LANES, (tile + 1) * LANES, CHUNK):
+                gathered = jnp.zeros((CHUNK, LANES), jnp.float32)
+                for block in range(4):
+                    for lane in range(TILES):
+                        ids = lax.broadcasted_iota(jnp.int32, (CHUNK, LANES), 1) + lane * LANES
+                        value = two_ref[block, pl.ds(start, CHUNK), pl.ds(lane * LANES, LANES)].astype(
+                            jnp.float32
+                        )
+                        gathered = gathered + jnp.where(
+                            ids < sizes_two_ref[block], value * value, 0.0
+                        )
+                summed.append(
+                    jnp.broadcast_to(jnp.sum(gathered, axis=1, keepdims=True), (CHUNK, LANES))
+                )
+            vectors_ref[pl.ds(12 + tile, 1), :] = jnp.sum(
+                jnp.where(diag, jnp.concatenate(summed, axis=0), 0.0), axis=0, keepdims=True
+            )
+
     slots, semaphores = plan_of_moves()
     work = items_of(slots)
     length = max(work) // 2 + 1
@@ -417,7 +441,7 @@
     order = [work[turn][1] for turn in sorted(work) if work[turn][0] == 0]
     fetches = [order[:4]] + [[step] for step in order[4:]] + [[]] * length
     whole = [max(turn // 2 for turn in work if work[turn][0] == part) for part in range(PARTS)]
-    extra = {}
+    extra = {5: [square_columns]}
     for part in range(PARTS - 1):
         for after, run in zip(AFTER[part], (first_start, first_onward, first_end)):
             extra.setdefault(min(whole[part] + after, length), []).append(
@@ -428,28 +452,6 @@
     moves(*slots[0], fetches[0])
     for copy in load_two:
         copy.start()
-    wait_bytes(two_ref, load_sem.at[1])
-    col_square = []
-    for tile in range(TILES):
-        summed = []
-        for start in range(tile * LANES, (tile + 1) * LANES, CHUNK):
-            gathered = jnp.zeros((CHUNK, LANES), jnp.float32)
-            for block in range(4):
-                for lane in range(TILES):
-                    ids = lax.broadcasted_iota(jnp.int32, (CHUNK, LANES), 1) + lane * LANES
-                    value = two_ref[block, pl.ds(start, CHUNK), pl.ds(lane * LANES, LANES)].astype(
-                        jnp.float32
-                    )
-                    gathered = gathered + jnp.where(
-                        ids < sizes_two_ref[block], value * value, 0.0
-                    )
-            summed.append(
-                jnp.broadcast_to(jnp.sum(gathered, axis=1, keepdims=True), (CHUNK, LANES))
-            )
-        vectors_ref[pl.ds(12 + tile, 1), :] = jnp.sum(
-            jnp.where(diag, jnp.concatenate(summed, axis=0), 0.0), axis=0, keepdims=True
-        )
-
     def one_slot(slot, carry):
         for group in range(0, length, 8):
 
@@ -626,7 +628,7 @@
             dma((2,)),
             dma((len(STEPS),)),
             dma((PARTS,)),
-            dma((len(plan_of_moves()[1]) + 4 * PARTS,)),
+            dma((len(plan_of_moves()[1]),)),
             dma((PARTS, len(STEPS))),
             dma((PARTS,)),
             dma((PARTS, 6)),

time: 115 us -> 114 us (level)
  no operation moved by 1% of the time
where the time goes in v5:
time: 114 us
  Pallas kernels  113 us (99%)
    pallas_call x1, Pallas kernels, body(): pl.pallas_call(functools.partial(gw_kernel, mass_scale), out_shape=(jax.S...  112 us

profile of v5, /device:TPU:1, one launch (start us, length us, event | category | flops | bytes accessed | tf_op | source)
XLA Modules:
  0.0 114.0 jit_solution(3210665206132029537)
XLA Ops:
  0.6 112.3 %gw_step.1 = (f32[512,512]{1,0:T(8,128)S(1)}, f32[512,128]{1,0:T(8,128)S(1)}, f32[16,128]{1,0:T(8,128)S(1)}) custom-call(bf16[512,16384]{1,0:T(8,128)(2,1)} %graph_one_ref.1, bf16[512,2048]{1,0:T(8,128)(2,1)} %graph_two_ref.1, f32[512,512]{1,0:T(8,128)} %coupling_ref.1, s32[32]{0:T(128)} %sizes_one_ref.1, s32[4]{0:T(128)} %sizes_two_ref.1), custom_call_target="tpu_custom_call" | custom-call | tf_op jit(solution)/shard_map/gw_step/pallas_call | solution.py:606
  112.9 1.1 finish.1

commit v6 on v5

--- a/solution.py
+++ b/solution.py
@@ -20,8 +20,10 @@
 STEPS = tuple((first, second) for second in OFFSETS for first in OFFSETS)
 HALF = BLOCK // 2
 UNIT = BLOCK // 4
-AFTER = ((1, 8, 40),)
-LAG = 2
+AFTER = ((7, 40),)
+LAG = 1
+LOOPED = 5
+CUTS = (1, 2)
 MESH = pl.DeviceIdType.MESH
 
 very_low = -1e30
@@ -135,8 +137,7 @@
             key = (part, STEPS.index((first, second)))
             count[key] = count.get(key, 0) + 1
             if count[key] == 4:
-                pace = 2 if part == 0 else 1
-                last = max(2 * (index + LAG), last + pace)
+                last = max(2 * (index + LAG), last + 1)
                 work[last] = key
     return work
 
@@ -219,16 +220,6 @@
                 graph_two_ref.at[:, pl.ds(block * BLOCK, BLOCK)], two_ref.at[block], load_sem.at[1]
             )
         )
-    total_one = jnp.float32(0)
-    for block in range(sizes_one_ref.shape[0]):
-        total_one = total_one + sizes_one_ref[block].astype(jnp.float32)
-    total_two = jnp.float32(0)
-    for block in range(sizes_two_ref.shape[0]):
-        total_two = total_two + sizes_two_ref[block].astype(jnp.float32)
-    all_one = jnp.full((TILES, LANES), total_one, jnp.float32)
-    all_two = jnp.full((TILES, LANES), total_two, jnp.float32)
-    log_one = jnp.log2(all_one)
-    log_two = jnp.log2(all_two)
     size_one = sizes_one_ref[row]
     size_two = sizes_two_ref[col]
     slot = lax.broadcasted_iota(jnp.int32, (TILES, LANES), 0) * LANES + lax.broadcasted_iota(
@@ -312,6 +303,24 @@
             value = jnp.where(index == place_of, options[offset % 4], value)
         return value
 
+    def add_products(plan, total_ref, chips):
+        for start in range(0, BLOCK, HALF):
+            total = total_ref[pl.ds(start, HALF), :]
+            for half in range(2):
+                rows = pl.ds(half * HALF, HALF)
+                for owner in (core, other):
+                    source = chips[half] + owner
+                    total = total + jnp.dot(
+                        one_ref[source, pl.ds(start, HALF), rows],
+                        plan[source, rows, :],
+                        preferred_element_type=jnp.float32,
+                    )
+            total_ref[pl.ds(start, HALF), :] = total
+
+    def multiply_slim(step, chips):
+        wait_bytes(plan_slim.at[0], pair_recv.at[1, step])
+        add_products(plan_slim, total_slim, chips)
+
     def multiply(code):
         part = jnp.where(code >= len(STEPS), 1, 0)
         step = code - len(STEPS) * part
@@ -321,30 +330,15 @@
         first = step - 4 * second
         chips = (pick(xs, first) + pick(zs, second), pick(xs, second) + pick(zs, first))
 
-        def add_products(plan, total_ref):
-            for start in range(0, BLOCK, HALF):
-                total = total_ref[pl.ds(start, HALF), :]
-                for half in range(2):
-                    rows = pl.ds(half * HALF, HALF)
-                    for owner in (core, other):
-                        source = chips[half] + owner
-                        total = total + jnp.dot(
-                            one_ref[source, pl.ds(start, HALF), rows],
-                            plan[source, rows, :],
-                            preferred_element_type=jnp.float32,
-                        )
-                total_ref[pl.ds(start, HALF), :] = total
-
         @pl.when(part > 0)
         def _():
-            wait_bytes(plan_slim.at[0], pair_recv.at[part, step])
-            add_products(plan_slim, total_slim)
+            multiply_slim(step, chips)
 
         @pl.when(part == 0)
         def _():
             wait_bytes(plan_wide.at[0], pair_recv.at[part, step])
             wait_bytes(one_ref.at[pl.ds(0, 2)], one_sem.at[step])
-            add_products(plan_wide, total_wide)
+            add_products(plan_wide, total_wide, chips)
             for start in range(0, BLOCK, CHUNK):
                 squares = squares_ref[pl.ds(start, CHUNK), :]
                 for half in range(2):
@@ -360,34 +354,43 @@
                             squares = squares + jnp.where(ids < size, value * value, 0.0)
                 squares_ref[pl.ds(start, CHUNK), :] = squares
 
-    def first_copy(part, half, source, key, target):
-        piece = firsts[part].at[source, pl.ds(half * HALF, HALF), :]
-        return pltpu.make_async_remote_copy(
+    def first_rows(part, half, cut):
+        if cut is None:
+            return pl.ds(half * HALF, HALF)
+        count = HALF // CUTS[part]
+        return pl.ds(half * HALF + cut * count, count)
+
+    def first_copy(part, half, cut, source, key, target):
+        piece = firsts[part].at[source, first_rows(part, half, cut), :]
+        pltpu.make_async_remote_copy(
             src_ref=piece,
             dst_ref=piece,
             send_sem=first_send.at[part],
             recv_sem=first_recv.at[part, key],
             device_id=(row, target),
             device_id_type=MESH,
-        )
+        ).start()
 
     def first_start(part):
         for start in range(0, BLOCK, CHUNK):
             rows = pl.ds(start, CHUNK)
             firsts[part][col, rows, :] = totals[part][rows, :].astype(jnp.bfloat16)
-        first_copy(part, 0, col, 0, up).start()
-        first_copy(part, 1, col, 1, down).start()
-        first_copy(part, 1, col, 2, up).start()
-        first_copy(part, 0, col, 3, down).start()
-
-    def first_wait(part, half, source, key):
-        wait_bytes(firsts[part].at[source, pl.ds(half * HALF, HALF), :], first_recv.at[part, key])
+        for cut in range(CUTS[part]):
+            first_copy(part, 0, cut, col, 4 + 2 * cut, up)
+            first_copy(part, 1, cut, col, 5 + 2 * cut, down)
+        first_copy(part, 1, None, col, 0, up)
+        first_copy(part, 0, None, col, 1, down)
+
+    def first_wait(part, half, cut, source, key):
+        piece = firsts[part].at[source, first_rows(part, half, cut), :]
+        wait_bytes(piece, first_recv.at[part, key])
 
     def first_onward(part):
-        first_wait(part, 0, down, 0)
-        first_copy(part, 0, down, 4, up).start()
-        first_wait(part, 1, up, 1)
-        first_copy(part, 1, up, 5, down).start()
+        for cut in range(CUTS[part]):
+            first_wait(part, 0, cut, down, 4 + 2 * cut)
+            first_copy(part, 0, cut, down, 2, up)
+            first_wait(part, 1, cut, up, 5 + 2 * cut)
+            first_copy(part, 1, cut, up, 3, down)
 
     def cross_add(part, source, fresh=False):
         added = lax.dot_general(
@@ -403,12 +406,12 @@
 
     def first_end(part):
         cross_add(part, col, fresh=part == 0)
-        first_wait(part, 1, down, 2)
+        first_wait(part, 1, None, down, 0)
         cross_add(part, down)
-        first_wait(part, 0, up, 3)
+        first_wait(part, 0, None, up, 1)
         cross_add(part, up)
-        first_wait(part, 0, across, 4)
-        first_wait(part, 1, across, 5)
+        first_wait(part, 0, None, across, 2)
+        first_wait(part, 1, None, across, 3)
         cross_add(part, across)
 
     def square_columns():
@@ -437,13 +440,14 @@
     slots, semaphores = plan_of_moves()
     work = items_of(slots)
     length = max(work) // 2 + 1
+    looped = max(turn // 2 for turn in work if work[turn][0] == 0) + 1 + LOOPED
     slots = slots + [([], [])] * (length - len(slots))
     order = [work[turn][1] for turn in sorted(work) if work[turn][0] == 0]
     fetches = [order[:4]] + [[step] for step in order[4:]] + [[]] * length
     whole = [max(turn // 2 for turn in work if work[turn][0] == part) for part in range(PARTS)]
     extra = {5: [square_columns]}
     for part in range(PARTS - 1):
-        for after, run in zip(AFTER[part], (first_start, first_onward, first_end)):
+        for after, run in zip(AFTER[part], (first_onward, first_end)):
             extra.setdefault(min(whole[part] + after, length), []).append(
                 functools.partial(run, part)
             )
@@ -452,12 +456,22 @@
     moves(*slots[0], fetches[0])
     for copy in load_two:
         copy.start()
+    total_one = jnp.float32(0)
+    for block in range(sizes_one_ref.shape[0]):
+        total_one = total_one + sizes_one_ref[block].astype(jnp.float32)
+    total_two = jnp.float32(0)
+    for block in range(sizes_two_ref.shape[0]):
+        total_two = total_two + sizes_two_ref[block].astype(jnp.float32)
+    all_one = jnp.full((TILES, LANES), total_one, jnp.float32)
+    all_two = jnp.full((TILES, LANES), total_two, jnp.float32)
+    log_one = jnp.log2(all_one)
+    log_two = jnp.log2(all_two)
     def one_slot(slot, carry):
-        for group in range(0, length, 8):
+        for group in range(0, looped, 8):
 
             @pl.when((slot >= group) & (slot < group + 8))
             def _():
-                for index in range(max(group, 1), min(group + 8, length)):
+                for index in range(max(group, 1), min(group + 8, looped)):
                     if slots[index] != ([], []) or fetches[index] or index in extra:
 
                         @pl.when(slot == index)
@@ -469,6 +483,8 @@
         def one_turn(turn, carry):
             code = jnp.int32(-1)
             for index, (part, step) in work.items():
+                if index >= 2 * looped:
+                    continue
                 code = jnp.where(2 * slot + turn == index, part * len(STEPS) + step, code)
 
             @pl.when(code >= 0)
@@ -477,9 +493,24 @@
 
             return carry
 
-        return lax.fori_loop(0, 2, one_turn, carry)
-
-    lax.fori_loop(0, length, one_slot, 0)
+        lax.fori_loop(0, 2, one_turn, 0)
+        for part in range(PARTS - 1):
+
+            @pl.when(slot == whole[part])
+            def _():
+                first_start(part)
+
+        return carry
+
+    lax.fori_loop(0, looped, one_slot, 0)
+    for index in range(looped, length):
+        moves(*slots[index], fetches[index])
+        for run in extra.get(index, ()):
+            run()
+        for turn in (2 * index, 2 * index + 1):
+            if turn in work:
+                step = work[turn][1]
+                multiply_slim(step, [place(half, *STEPS[step]) - core for half in range(2)])
     first_start(PARTS - 1)
     for run in extra.get(length, ()):
         run()
@@ -520,6 +551,7 @@
         return jnp.concatenate([gamma[t : t + 1, :] for t in range(TILES)], axis=1)
 
     def sweep_body(sweep, gamma):
+        lines = []
         for tile in range(TILES):
             column = []
             for start in range(tile * LANES, (tile + 1) * LANES, CHUNK):
@@ -528,19 +560,24 @@
                 summed = jnp.sum(jnp.exp2(values - top), axis=1, keepdims=True)
                 column.append(jnp.broadcast_to(top + jnp.log2(summed), (CHUNK, LANES)))
             column = jnp.concatenate(column, axis=0)
-            row_box[sweep, col, pl.ds(tile, 1), :] = jnp.sum(
-                jnp.where(diag, column, 0.0), axis=0, keepdims=True
-            )
+            lines.append(jnp.sum(jnp.where(diag, column, 0.0), axis=0, keepdims=True))
+        row_box[sweep, col] = jnp.concatenate(lines, axis=0)
         lse = exchange(
             row_box, col, sweep, row_send, row_recv, [(row, peer) for peer in row_peers]
         )
         rho = jnp.where(live_row, -log_one - lse, 0.0)
         vectors_ref[pl.ds(0, TILES), :] = rho
+        columns = []
         for tile in range(TILES):
             spread = jnp.broadcast_to(rho[tile : tile + 1, :], (LANES, LANES))
+            columns.append(
+                jnp.sum(jnp.where(diag, spread, 0.0), axis=1, keepdims=True)
+            )
+        for tile in range(TILES):
             rho_ref[pl.ds(tile * LANES, LANES), :] = jnp.broadcast_to(
-                jnp.sum(jnp.where(diag, spread, 0.0), axis=1, keepdims=True), (LANES, LANES)
+                columns[tile], (LANES, LANES)
             )
+        lines = []
         for tile in range(TILES):
             lanes = pl.ds(tile * LANES, LANES)
             tops, sums = [], []
@@ -555,9 +592,8 @@
             high = functools.reduce(jnp.maximum, tops)
             high = jnp.max(high, axis=0, keepdims=True)
             summed = sum(s * jnp.exp2(t - high) for s, t in zip(sums, tops))
-            col_box[sweep, row, pl.ds(tile, 1), :] = high + jnp.log2(
-                jnp.sum(summed, axis=0, keepdims=True)
-            )
+            lines.append(high + jnp.log2(jnp.sum(summed, axis=0, keepdims=True)))
+        col_box[sweep, row] = jnp.concatenate(lines, axis=0)
         lse = exchange(
             col_box, row, sweep, col_send, col_recv, [(peer, col) for peer in col_peers]
         )
@@ -580,16 +616,26 @@
         wait_bytes(firsts[part].at[pl.ds(0, 3)], first_send.at[part])
 
 
-def finish_kernel(mass_scale, cost_ref, rho_ref, vectors_ref, plan_ref, row_ref, col_ref):
+def finish_kernel(
+    mass_scale, cost_ref, rho_ref, vectors_ref, plan_ref, row_ref, col_ref, made_ref, made_sem
+):
     gamma = jnp.concatenate([vectors_ref[pl.ds(4 + t, 1), :] for t in range(TILES)], axis=1)
-    for start in range(0, BLOCK, CHUNK):
-        rows = pl.ds(start, CHUNK)
+    copies = []
+    for start in range(0, BLOCK, LANES):
+        rows = pl.ds(start, LANES)
         exponent = (
             cost_ref[rows, :] + jnp.concatenate([rho_ref[rows, :]] * TILES, axis=1) + gamma
         )
-        plan_ref[rows, :] = jnp.float32(mass_scale) * jnp.exp2(exponent)
+        made_ref[rows, :] = jnp.float32(mass_scale) * jnp.exp2(exponent)
+        copy = pltpu.make_async_copy(
+            made_ref.at[rows, :], plan_ref.at[rows, :], made_sem.at[start // LANES]
+        )
+        copy.start()
+        copies.append(copy)
     row_ref[...] = vectors_ref[pl.ds(8, TILES), :]
     col_ref[...] = vectors_ref[pl.ds(12, TILES), :]
+    for copy in copies:
+        copy.wait()
 
 
 def body(graph_one, graph_two, coupling, sizes_one, sizes_two):
@@ -631,7 +677,7 @@
             dma((len(plan_of_moves()[1]),)),
             dma((PARTS, len(STEPS))),
             dma((PARTS,)),
-            dma((PARTS, 6)),
+            dma((PARTS, 4 + 2 * max(CUTS))),
             dma((1,)),
             dma((SWEEPS,)),
             dma((1,)),
@@ -650,7 +696,8 @@
             jax.ShapeDtypeStruct((TILES, LANES), f32),
         ),
         in_specs=[vmem, vmem, vmem],
-        out_specs=(vmem, vmem, vmem),
+        out_specs=(hbm, vmem, vmem),
+        scratch_shapes=[pltpu.VMEM((BLOCK, BLOCK), f32), dma((TILES,))],
         compiler_params=pltpu.CompilerParams(vmem_limit_bytes=8 * 1024 * 1024),
         name="finish",
     )(cost, rho, vectors)

time: 114 us -> 114 us (level)
  no operation moved by 1% of the time
where the time goes in v6:
time: 114 us
  Pallas kernels  113 us (99%)
    pallas_call x1, Pallas kernels, body(): pl.pallas_call(functools.partial(gw_kernel, mass_scale), out_shape=(jax.S...  112 us

profile of v6, /device:TPU:1, one launch (start us, length us, event | category | flops | bytes accessed | tf_op | source)
XLA Modules:
  0.0 114.0 jit_solution(14835281506367980068)
XLA Ops:
  0.6 111.7 %gw_step.1 = (f32[512,512]{1,0:T(8,128)S(1)}, f32[512,128]{1,0:T(8,128)S(1)}, f32[16,128]{1,0:T(8,128)S(1)}) custom-call(bf16[512,16384]{1,0:T(8,128)(2,1)} %graph_one_ref.1, bf16[512,2048]{1,0:T(8,128)(2,1)} %graph_two_ref.1, f32[512,512]{1,0:T(8,128)} %coupling_ref.1, s32[32]{0:T(128)} %sizes_one_ref.1, s32[4]{0:T(128)} %sizes_two_ref.1), custom_call_target="tpu_custom_call" | custom-call | tf_op jit(solution)/shard_map/gw_step/pallas_call | solution.py:652
  112.3 1.6 %finish.1 = (f32[512,512]{1,0:T(8,128)}, f32[4,128]{1,0:T(4,128)}, f32[4,128]{1,0:T(4,128)}) custom-call(f32[512,512]{1,0:T(8,128)S(1)} %get-tuple-element.9.cost_ref, f32[512,128]{1,0:T(8,128)S(1)} %get-tuple-element.10.rho_ref, f32[16,128]{1,0:T(8,128)S(1)} %get-tuple-element.11.vectors_ref), custom_call_target="tpu_custom_call" | custom-call | tf_op jit(solution)/shard_map/finish/pallas_call | solution.py:691

commit v7 on v6

--- a/solution.py
+++ b/solution.py
@@ -23,7 +23,7 @@
 AFTER = ((7, 40),)
 LAG = 1
 LOOPED = 5
-CUTS = (1, 2)
+CUTS = (1, 4)
 MESH = pl.DeviceIdType.MESH
 
 very_low = -1e30

time: 114 us -> 114 us (level)
  no operation moved by 1% of the time
where the time goes in v7:
time: 114 us
  Pallas kernels  113 us (99%)
    pallas_call x1, Pallas kernels, body(): pl.pallas_call(functools.partial(gw_kernel, mass_scale), out_shape=(jax.S...  112 us

profile of v7, /device:TPU:1, one launch (start us, length us, event | category | flops | bytes accessed | tf_op | source)
XLA Modules:
  0.0 113.8 jit_solution(9370042556345756767)
XLA Ops:
  0.6 111.6 %gw_step.1 = (f32[512,512]{1,0:T(8,128)S(1)}, f32[512,128]{1,0:T(8,128)S(1)}, f32[16,128]{1,0:T(8,128)S(1)}) custom-call(bf16[512,16384]{1,0:T(8,128)(2,1)} %graph_one_ref.1, bf16[512,2048]{1,0:T(8,128)(2,1)} %graph_two_ref.1, f32[512,512]{1,0:T(8,128)} %coupling_ref.1, s32[32]{0:T(128)} %sizes_one_ref.1, s32[4]{0:T(128)} %sizes_two_ref.1), custom_call_target="tpu_custom_call" | custom-call | tf_op jit(solution)/shard_map/gw_step/pallas_call | solution.py:652
  112.2 1.6 %finish.1 = (f32[512,512]{1,0:T(8,128)}, f32[4,128]{1,0:T(4,128)}, f32[4,128]{1,0:T(4,128)}) custom-call(f32[512,512]{1,0:T(8,128)S(1)} %get-tuple-element.9.cost_ref, f32[512,128]{1,0:T(8,128)S(1)} %get-tuple-element.10.rho_ref, f32[16,128]{1,0:T(8,128)S(1)} %get-tuple-element.11.vectors_ref), custom_call_target="tpu_custom_call" | custom-call | tf_op jit(solution)/shard_map/finish/pallas_call | solution.py:691
